TPU v7x, 16 devices: a 4x2x1 block of a 4x4x8 slice. The times are simulated.
16 devices in a mesh: dp: 2 (over y, z), dpa: 8 (over x, core).
Axes of the slice: x: 4, y: 2, z: 1, core: 2. Of those that a mesh axis runs over, the one named last changes fastest.
The devices are a block of a 4x4x8 slice.
Arguments:
- x: bfloat16 [16, 4, 512, 2048], P(('dp', 'dpa')), parts along dimension 0
- chunk_len: int32 [16, 4], P(('dp', 'dpa')), parts along dimension 0
- ctx_len: int32 [16, 4], P(('dp', 'dpa')), parts along dimension 0
- lat_cache: bfloat16 [16, 4, 1024, 512], P(('dp', 'dpa')), parts along dimension 0
- rope_cache: bfloat16 [16, 4, 1024, 64], P(('dp', 'dpa')), parts along dimension 0
- topk_idx: int32 [16, 4, 512, 6], P(('dp', 'dpa')), parts along dimension 0
- g_attn: bfloat16 [2048], replicated
- w_q: bfloat16 [2048, 16, 192], replicated
- w_dkv: bfloat16 [2048, 512], replicated
- g_kv: bfloat16 [512], replicated
- w_kr: bfloat16 [2048, 64], replicated
- w_uk: bfloat16 [512, 16, 128], replicated
- w_uv: bfloat16 [512, 16, 128], replicated
- w_o: bfloat16 [16, 128, 2048], replicated
- g_ffn: bfloat16 [2048], replicated
- w_router: bfloat16 [2048, 64], replicated
- w_sh_gate: bfloat16 [2048, 2816], replicated
- w_sh_up: bfloat16 [2048, 2816], replicated
- w_sh_down: bfloat16 [2816, 2048], replicated
- w_exp_gate: bfloat16 [64, 2048, 1408], P('dpa')
- w_exp_up: bfloat16 [64, 2048, 1408], P('dpa')
- w_exp_down: bfloat16 [64, 1408, 2048], P('dpa')
Outputs:
- output 1: bfloat16 [16, 4, 512, 2048], P(('dp', 'dpa')), parts along dimension 0
- output 2: bfloat16 [16, 4, 1024, 512], P(('dp', 'dpa')), parts along dimension 0
- output 3: bfloat16 [16, 4, 1024, 64], P(('dp', 'dpa')), parts along dimension 0
There are 2 independent parts. A program takes and returns all parts, laid end to end along the dimension named above; an argument that names none is the same for every part.
All inputs are finite; a program needn't handle non-finite values.
Results may differ from a plain program's by a relative error of at most 0.0196382.
Values are sent between devices in bfloat16 or wider.
A program may use at most 768 MiB of HBM per device.

v0:
```python
import jax
import jax.numpy as jnp
from jax import lax
from jax.sharding import PartitionSpec as P

EPS = 1e-6
THETA = 10000.0


def rms_norm(vals, gain):
    vals_f32 = vals.astype(jnp.float32)
    inv_rms = lax.rsqrt(jnp.mean(vals_f32 * vals_f32, axis=-1, keepdims=True) + EPS)
    return (vals_f32 * inv_rms * gain.astype(jnp.float32)).astype(jnp.bfloat16)


def rope_tables(positions, half):
    inv_freq = THETA ** (-2.0 * jnp.arange(half, dtype=jnp.float32) / (2 * half))
    angle = positions.astype(jnp.float32)[..., None] * inv_freq
    return jnp.cos(angle), jnp.sin(angle)


def rotate(vals, cos_tab, sin_tab):
    half = cos_tab.shape[-1]
    first = vals[..., :half]
    second = vals[..., half:]
    return jnp.concatenate([first * cos_tab - second * sin_tab, second * cos_tab + first * sin_tab], axis=-1)


def write_window(cache_row, new_rows, start, keep):
    old_rows = lax.dynamic_slice_in_dim(cache_row, start, new_rows.shape[0], axis=0)
    merged = jnp.where(keep[:, None], new_rows, old_rows)
    return lax.dynamic_update_slice_in_dim(cache_row, merged, start, axis=0)


def attention_block(x_in, chunk_len, ctx_len, lat_cache, rope_cache, g_attn, w_q, w_dkv, g_kv, w_kr, w_uk, w_uv, w_o):
    chunk = x_in.shape[2]
    ctx_max = lat_cache.shape[2]
    rope_dim = w_kr.shape[1]
    nope_dim = w_q.shape[2] - rope_dim
    scale = w_q.shape[2] ** -0.5
    normed = rms_norm(x_in, g_attn)
    q_full = jnp.einsum('brcd,dhq->brchq', normed, w_q, preferred_element_type=jnp.float32).astype(jnp.bfloat16)
    positions = ctx_len[:, :, None] + jnp.arange(chunk)
    cos_tab, sin_tab = rope_tables(positions, rope_dim // 2)
    q_rope = rotate(q_full[..., nope_dim:].astype(jnp.float32), cos_tab[..., None, :], sin_tab[..., None, :]).astype(jnp.bfloat16)
    q_lat = jnp.einsum('brchn,khn->brchk', q_full[..., :nope_dim], w_uk, preferred_element_type=jnp.float32).astype(jnp.bfloat16)
    lat_new = rms_norm(jnp.einsum('brcd,dk->brck', normed, w_dkv, preferred_element_type=jnp.float32), g_kv)
    rope_new = rotate(jnp.einsum('brcd,dp->brcp', normed, w_kr, preferred_element_type=jnp.float32), cos_tab, sin_tab).astype(jnp.bfloat16)
    keep = jnp.arange(chunk) < chunk_len[:, :, None]
    writer = jax.vmap(jax.vmap(write_window))
    lat_upd = writer(lat_cache, lat_new, ctx_len, keep)
    rope_upd = writer(rope_cache, rope_new, ctx_len, keep)
    key_pos = jnp.arange(ctx_max)

    def one_request(index):
        q_lat_req = lax.dynamic_index_in_dim(q_lat, index, axis=1, keepdims=False)
        q_rope_req = lax.dynamic_index_in_dim(q_rope, index, axis=1, keepdims=False)
        lat_req = lax.dynamic_index_in_dim(lat_upd, index, axis=1, keepdims=False)
        rope_req = lax.dynamic_index_in_dim(rope_upd, index, axis=1, keepdims=False)
        pos_req = lax.dynamic_index_in_dim(positions, index, axis=1, keepdims=False)
        scores = (jnp.einsum('bchk,blk->bchl', q_lat_req, lat_req, preferred_element_type=jnp.float32) + jnp.einsum('bchp,blp->bchl', q_rope_req, rope_req, preferred_element_type=jnp.float32)) * scale
        visible = key_pos[None, None, None, :] <= pos_req[:, :, None, None]
        scores = jnp.where(visible, scores, -1e30)
        attn_prob = jax.nn.softmax(scores, axis=-1).astype(jnp.bfloat16)
        return jnp.einsum('bchl,blk->bchk', attn_prob, lat_req, preferred_element_type=jnp.float32).astype(jnp.bfloat16)

    out_lat = lax.map(one_request, jnp.arange(x_in.shape[1]))
    out_head = jnp.einsum('rbchk,khv->brchv', out_lat, w_uv, preferred_element_type=jnp.float32).astype(jnp.bfloat16)
    attn_out = jnp.einsum('brchv,hvd->brcd', out_head, w_o, preferred_element_type=jnp.float32).astype(jnp.bfloat16)
    hidden = (x_in.astype(jnp.float32) + attn_out.astype(jnp.float32)).astype(jnp.bfloat16)
    return hidden, lat_upd, rope_upd


def router_and_shared(hidden_rows, g_ffn, w_router, w_sh_gate, w_sh_up, w_sh_down):
    normed = rms_norm(hidden_rows, g_ffn)
    route_prob = jax.nn.softmax(jnp.dot(normed, w_router, preferred_element_type=jnp.float32), axis=-1)
    shared_act = (jax.nn.silu(jnp.dot(normed, w_sh_gate, preferred_element_type=jnp.float32)) * jnp.dot(normed, w_sh_up, preferred_element_type=jnp.float32)).astype(jnp.bfloat16)
    shared_out = jnp.dot(shared_act, w_sh_down, preferred_element_type=jnp.float32)
    return normed, route_prob, shared_out


def expert_ffn(sorted_rows, sizes, w_exp_gate, w_exp_up, w_exp_down):
    gate_part = lax.ragged_dot(sorted_rows, w_exp_gate, sizes, preferred_element_type=jnp.float32)
    up_part = lax.ragged_dot(sorted_rows, w_exp_up, sizes, preferred_element_type=jnp.float32)
    act = (jax.nn.silu(gate_part) * up_part).astype(jnp.bfloat16)
    return lax.ragged_dot(act, w_exp_down, sizes, preferred_element_type=jnp.float32).astype(jnp.bfloat16)


def solution(mesh):
    group = mesh.shape['dpa']
    tok_spec = P(('dp', 'dpa'))
    whole = P()
    exp_spec = P('dpa')

    def device_step(x_in, chunk_len, ctx_len, lat_cache, rope_cache, topk_idx, g_attn, w_q, w_dkv, g_kv, w_kr, w_uk, w_uv, w_o, g_ffn, w_router, w_sh_gate, w_sh_up, w_sh_down, w_exp_gate, w_exp_up, w_exp_down):
        hidden, lat_upd, rope_upd = attention_block(x_in, chunk_len, ctx_len, lat_cache, rope_cache, g_attn, w_q, w_dkv, g_kv, w_kr, w_uk, w_uv, w_o)
        chunk = hidden.shape[2]
        width = hidden.shape[3]
        tokens = hidden.shape[1] * chunk
        top_k = topk_idx.shape[-1]
        local_exp = w_exp_gate.shape[0]
        capacity = tokens * top_k // group
        flat_h = hidden.reshape(tokens, width)
        normed, route_prob, shared_out = router_and_shared(flat_h, g_ffn, w_router, w_sh_gate, w_sh_up, w_sh_down)
        valid = (jnp.arange(chunk)[None, :] < chunk_len[0][:, None]).reshape(tokens)
        choice = topk_idx.reshape(tokens, top_k)
        gates = jnp.take_along_axis(route_prob, choice, axis=1)
        flat_choice = choice.reshape(tokens * top_k)
        target = flat_choice // local_exp
        hits = (target[:, None] == jnp.arange(group)[None, :]).astype(jnp.int32)
        rank_in = jnp.sum(jnp.cumsum(hits, axis=0) * hits, axis=1) - 1
        slot = target * capacity + rank_in
        pair_of_slot = jnp.argsort(slot)
        pair_valid = jnp.repeat(valid, top_k)
        expert_key = jnp.where(pair_valid, flat_choice % local_exp, local_exp).astype(jnp.int32)
        send_rows = normed[pair_of_slot // top_k]
        send_key = expert_key[pair_of_slot]
        recv_rows = lax.all_to_all(send_rows, 'dpa', 0, 0, tiled=True)
        recv_key = lax.all_to_all(send_key, 'dpa', 0, 0, tiled=True)
        order = jnp.argsort(recv_key, stable=True)
        sizes = jnp.bincount(recv_key, length=local_exp + 1)[:local_exp].astype(jnp.int32)
        sorted_out = expert_ffn(recv_rows[order], sizes, w_exp_gate, w_exp_up, w_exp_down)
        expert_rows = sorted_out[jnp.argsort(order)]
        back_rows = lax.all_to_all(expert_rows, 'dpa', 0, 0, tiled=True)
        pair_out = back_rows[slot].reshape(tokens, top_k, width)
        routed = jnp.sum(gates[:, :, None] * pair_out.astype(jnp.float32), axis=1)
        total = flat_h.astype(jnp.float32) + shared_out + routed
        result = jnp.where(valid[:, None], total, 0.0).astype(jnp.bfloat16)
        return result.reshape(hidden.shape), lat_upd, rope_upd

    return jax.shard_map(device_step, mesh=mesh, in_specs=(tok_spec,) * 6 + (whole,) * 13 + (exp_spec,) * 3, out_specs=(tok_spec, tok_spec, tok_spec), check_vma=False)
```

profile of v0, /device:TPU:112, one launch (start us, length us, event | category | flops | bytes accessed | tf_op | source)
XLA Modules:
  0.0 3284.1 jit_solution(11257541256831911688)
XLA Ops:
  23.5 8.2 sort.48
  32.4 120.4 %gather_fusion.1 = s32[12288]{0:T(1024)} fusion(s32[12288]{0:T(1024)S(1)} %get-tuple-element.205, s32[12288]{0:T(1024)S(1)} %get-tuple-element.207), kind=kCustom, calls=%fused_computation.1 | custom fusion | bytes 147456 | tf_op jit(solution)/shard_map/gather | solution.py:117
  152.8 5.7 all-to-all-start.1
  182.6 38.5 %while.16 = (s32[]{:T(128)}, bf16[1,4,1024,64]{2,3,1,0:T(8,128)(2,1)}, s32[4,4]{1,0:T(4,128)S(1)}, bf16[4,512,64]{1,2,0:T(8,128)(2,1)S(1)}, s32[]{:T(128)}, /*index=5*/s32[4]{0:T(128)S(1)}, s32[]{:T(128)}) while((s32[]{:T(128)}, bf16[1,4,1024,64]{2,3,1,0:T(8,128)(2,1)}, s32[4,4]{1,0:T(4,128)S(1)}, bf16[4,512,64]{1,2,0:T(8,128)(2,1)S(1)}, s32[]{:T(128)}, ...), condition=%wide.while_cond.2, body=%wide.while_body.2.sunk | while | flops 32797 | bytes 327875 | solution.py:32
  221.0 31.9 convert_bitcast_fusion.1
  262.0 16.8 while.14
  278.9 8.1 multiply_reduce_fusion.1
  289.1 56.5 %while.15 = (s32[]{:T(128)}, bf16[1,4,1024,512]{3,2,1,0:T(8,128)(2,1)}, s32[4,4]{1,0:T(4,128)}, bf16[4,512,512]{1,2,0:T(8,128)(2,1)}, s32[]{:T(128)}, /*index=5*/s32[4]{0:T(128)S(1)}, s32[]{:T(128)}) while((s32[]{:T(128)}, bf16[1,4,1024,512]{3,2,1,0:T(8,128)(2,1)}, s32[4,4]{1,0:T(4,128)}, bf16[4,512,512]{1,2,0:T(8,128)(2,1)}, s32[]{:T(128)}, ...), condition=%wide.while_cond.1, body=%wide.while_body.1.sunk | while | flops 262173 | bytes 4718787 | solution.py:32
  345.6 18.3 convert_bitcast_fusion
  371.4 258.0 %while.17 = (s32[]{:T(128)}, bf16[4,1,512,16,512]{4,2,3,1,0:T(8,128)(2,1)}, s32[4]{0:T(128)S(1)}, s32[1,4,512]{2,1,0:T(4,128)S(1)}, bf16[1,4,512,16,512]{4,2,1,3...) while((s32[]{:T(128)}, ...), condition=%wide.region_7.8_spmd.clone, body=%wide.region_4.7_spmd.clone.sunk | while | flops 18317049856 | bytes 155394736 | solution.py:67
  374.2 17.8 fusion.177
  392.4 26.1 fusion.178
  418.5 17.5 bitcast_dynamic-update-slice_fusion.2
  438.6 17.8 fusion.177
  456.8 26.1 fusion.178
  482.9 17.4 bitcast_dynamic-update-slice_fusion.2
  503.0 17.8 fusion.177
  521.2 26.1 fusion.178
  547.3 17.4 bitcast_dynamic-update-slice_fusion.2
  567.4 17.8 fusion.177
  585.6 26.1 fusion.178
  611.7 17.4 bitcast_dynamic-update-slice_fusion.2
  629.4 18.8 fusion.72.clone.4
  648.2 24.3 fusion.39
  672.5 8.8 fusion.41
  681.3 95.8 %gather_fusion = bf16[12288,2048]{1,0:T(8,128)(2,1)} fusion(bf16[2048,2048]{1,0:T(8,128)(2,1)} %fusion.41, s32[12288]{0:T(1024)S(1)} %copy-done.13), kind=kCustom, calls=%fused_computation | custom fusion | bytes 100712448 | tf_op jit(solution)/shard_map/gather | solution.py:116
  777.1 8.7 all-to-all-start
  786.7 85.8 %scatter_custom_fusion = s32[9]{0:T(128)} fusion(s32[12288]{0:T(1024)S(1)} %bitcast.292, s32[12288]{0:T(1024)S(1)} %ne.62, s32[]{:T(128)} %constant.85.clone.1), kind=kCustom, calls=%fused_computation.180 | custom fusion | flops 12288 | bytes 40 | tf_op jit(solution)/shard_map/scatter-add | solution.py:121
  874.8 9.0 sort.49
  883.8 8.2 sort.50
  892.6 437.2 %all-to-all-done = bf16[8,1536,2048]{2,1,0:T(8,128)(2,1)} async-done(((bf16[8,1536,2048]{2,1,0:T(8,128)(2,1)}), bf16[8,1536,2048]{2,1,0:T(8,128)(2,1)}, u32[]{:S(2)}, u32[]{:S(2)}) %all-to-all-start) | async-done | bytes 50331680 | tf_op jit(solution)/shard_map/all_to_all | solution.py:118
  1329.7 286.4 %gather_fusion.2 = bf16[12288,2048]{1,0:T(8,128)(2,1)} fusion(bf16[12288,2048]{1,0:T(8,128)(2,1)} %bitcast.36, s32[12288]{0:T(1024)S(1)} %fusion.103), kind=kCustom, calls=%fused_computation.2 | custom fusion | bytes 100712448 | tf_op jit(solution)/shard_map/gather | solution.py:122
  1616.1 83.0 %ragged-dot-none.2 = f32[12288,1408]{1,0:T(8,128)} custom-call(s32[1]{0:T(128)} %get-tuple-element.81, s32[9]{0:T(128)} %get-tuple-element.82, s32[55]{0:T(128)} %get-tuple-element.83, s32[55]{0:T(128)} %get-tuple-element.84, s32[1]{0:T(128)} %get-tuple-element.81, bf16[12288,2048]{1,0:T(8,128)(2,1)} %gather_fusion.2, bf16[8,2048,1408]{2,1,0:T(8,128)(2,1)} %param.43), custom_call_target="tpu_custom_call" | custom-call | flops 70866960384 | bytes 165675040 | tf_op jit(solution)/shard_map/ragged_dot_general/ragged-dot-none
  1699.2 83.1 %ragged-dot-none.1 = f32[12288,1408]{1,0:T(8,128)} custom-call(s32[1]{0:T(128)} %get-tuple-element.81, s32[9]{0:T(128)} %get-tuple-element.82, s32[55]{0:T(128)} %get-tuple-element.83, s32[55]{0:T(128)} %get-tuple-element.84, s32[1]{0:T(128)} %get-tuple-element.81, bf16[12288,2048]{1,0:T(8,128)(2,1)} %gather_fusion.2, bf16[8,2048,1408]{2,1,0:T(8,128)(2,1)} %param.44), custom_call_target="tpu_custom_call" | custom-call | flops 70866960384 | bytes 165675040 | tf_op jit(solution)/shard_map/ragged_dot_general/ragged-dot-none
  1782.2 55.0 %multiply_convert_fusion = bf16[12288,1408]{1,0:T(8,128)(2,1)} fusion(f32[12288,1408]{1,0:T(8,128)} %ragged-dot-none.1, f32[12288,1408]{1,0:T(8,128)} %ragged-dot-none.2), kind=kLoop, calls=%fused_computation.48 | loop fusion | flops 103809024 | bytes 173015040 | tf_op jit(solution)/shard_map/convert_element_type | solution.py:85
  1837.2 84.6 %ragged-dot-none = f32[12288,2048]{1,0:T(8,128)} custom-call(s32[1]{0:T(128)} %get-tuple-element.81, s32[9]{0:T(128)} %get-tuple-element.82, s32[55]{0:T(128)} %get-tuple-element.83, s32[55]{0:T(128)} %get-tuple-element.84, s32[1]{0:T(128)} %get-tuple-element.81, bf16[12288,1408]{1,0:T(8,128)(2,1)} %multiply_convert_fusion, bf16[8,1408,2048]{2,1,0:T(8,128)(2,1)} %param.45), custom_call_target="tpu_custom_call" | custom-call | flops 70866960384 | bytes 181403680 | tf_op jit(solution)/shard_map/ragged_dot_general/ragged-dot-none
  1921.8 48.0 %convert_element_type.166 = bf16[12288,2048]{1,0:T(8,128)(2,1)} convert(f32[12288,2048]{1,0:T(8,128)} %ragged-dot-none) | non-fusion elementwise | flops 25165824 | bytes 150994944 | tf_op jit(solution)/shard_map/convert_element_type | solution.py:86
  1969.9 286.4 %gather_fusion.3 = bf16[12288,2048]{1,0:T(8,128)(2,1)} fusion(bf16[12288,2048]{1,0:T(8,128)(2,1)} %convert_element_type.166, s32[12288]{0:T(1024)S(1)} %copy-done.11), kind=kCustom, calls=%fused_computation.3 | custom fusion | bytes 100712448 | tf_op jit(solution)/shard_map/gather | solution.py:123
  2256.2 9.1 all-to-all-start.2
  2268.0 6.0 fusion.131
  2274.3 98.0 %gather_fusion.6 = f32[12288]{0:T(1024)S(1)} fusion(f32[2048,64]{0,1:T(8,128)S(1)} %fusion.84, s32[12288]{0:T(1024)S(1)} %reshape.742), kind=kCustom, calls=%fused_computation.6 | custom fusion | bytes 196608 | tf_op jit(solution)/shard_map/jit(take_along_axis)/gather | solution.py:107
  2375.5 31.8 fusion.132
  2407.4 34.6 %multiply_convert_fusion.1.clone.6 = bf16[2048,2816]{1,0:T(8,128)(2,1)} fusion(f32[2048,2816]{1,0:T(8,128)} %fusion.132, bf16[2048,2048]{1,0:T(8,128)(2,1)} %fusion.41, bf16[2048,2816]{1,0:T(8,128)(2,1)} %param.41), kind=kOutput, calls=%fused_computation.55.clone.clone.clone.clone.clone.1 | convolution fusion | flops 23656923136 | bytes 54525952 | tf_op jit(solution)/shard_map/dot_general | solution.py:77
  2442.0 367.1 %all-to-all-done.2 = bf16[8,1536,2048]{2,1,0:T(8,128)(2,1)} async-done(((bf16[8,1536,2048]{2,1,0:T(8,128)(2,1)}), bf16[8,1536,2048]{2,1,0:T(8,128)(2,1)}, u32[]{:S(2)}, u32[]{:S(2)}) %all-to-all-start.2) | async-done | bytes 50331680 | tf_op jit(solution)/shard_map/all_to_all | solution.py:124
  2809.1 286.3 %gather_fusion.4 = bf16[12288,2048]{1,0:T(8,128)(2,1)} fusion(bf16[12288,2048]{1,0:T(8,128)(2,1)} %bitcast.39, s32[12288]{0:T(1024)S(1)} %copy-done.12), kind=kCustom, calls=%fused_computation.4 | custom fusion | bytes 100712448 | tf_op jit(solution)/shard_map/gather | solution.py:125
  3095.4 84.5 %reshape.693 = f32[2048,6,2048]{2,1,0:T(8,128)} reshape(bf16[12288,2048]{1,0:T(8,128)(2,1)} %gather_fusion.4) | data formatting | bytes 150994944 | tf_op jit(solution)/shard_map/convert_element_type | solution.py:126
  3179.9 69.5 %multiply_reduce_fusion = f32[2048,2048]{1,0:T(8,128)} fusion(f32[2048,6,2048]{2,1,0:T(8,128)} %reshape.693, f32[2048,6]{1,0:T(8,128)S(1)} %copy-done.7), kind=kLoop, calls=%fused_computation.47 | loop fusion | flops 46137344 | bytes 117489664 | tf_op jit(solution)/shard_map/reduce_sum | solution.py:126
  3249.5 34.2 %fusion.44 = bf16[2048,2048]{1,0:T(8,128)(2,1)} fusion(f32[2048,2048]{1,0:T(8,128)} %multiply_reduce_fusion, bf16[1,4,512,2048]{3,2,1,0:T(8,128)(2,1)S(1)} %copy-done.6, pred[2048]{0:T(1024)(128)(4,1)S(1)} %bitcast.296, bf16[2816,2048]{1,0:T(8,128)(2,1)} %param.42, bf16[2048,2816]{1,0:T(8,128)(2,1)} %multiply_convert_fusion.1.clone.6), kind=kOutput, calls=%fused_computation.68 | convolution fusion | flops 23643291648 | bytes 56625152 | tf_op jit(solution)/shard_map/dot_general | solution.py:78
  (218 shorter events, 191.5 us)
Async XLA Ops:
  0.6 345.0 %copy-start = (bf16[512,16,128]{2,1,0:T(8,128)(2,1)S(1)}, bf16[512,16,128]{2,1,0:T(8,128)(2,1)}, u32[]{:S(2)}) copy-start(bf16[512,16,128]{2,1,0:T(8,128)(2,1)} %param.35) | copy-start | bytes 6291460
  0.6 9.7 copy-start.30
  8.3 12.4 copy-start.2
  18.9 0.6 copy-start.19
  32.4 126.1 %copy-start.27 = (s32[1,4]{1,0:T(1,128)S(1)}, s32[1,4]{1,0:T(1,128)}, u32[]{:S(2)}) copy-start(s32[1,4]{1,0:T(1,128)} %param.26) | copy-start | bytes 52
  32.4 131.3 %copy-start.25 = (bf16[2048]{0:T(1024)(128)(2,1)S(1)}, bf16[2048]{0:T(1024)(128)(2,1)}, u32[]{:S(2)}) copy-start(bf16[2048]{0:T(1024)(128)(2,1)} %param.30) | copy-start | bytes 12292
  32.4 133.1 %copy-start.32 = (bf16[2048,64]{0,1:T(8,128)(2,1)S(1)}, bf16[2048,64]{0,1:T(8,128)(2,1)}, u32[]{:S(2)}) copy-start(bf16[2048,64]{0,1:T(8,128)(2,1)} %param.34) | copy-start | bytes 786436
  152.8 624.3 %all-to-all-start.1 = ((s32[8,1536,1]{1,2,0:T(1,128)}), s32[8,1536,1]{1,2,0:T(1,128)}, u32[]{:S(2)}, u32[]{:S(2)}) async-start(s32[8,1536,1]{1,2,0:T(1,128)} %bitcast.33), calls=%async_computation.1 | async-start | bytes 98304 | tf_op jit(solution)/shard_map/all_to_all | solution.py:119
  163.8 1.8 copy-start.23
  163.8 1.8 copy-start.21
  165.6 7.0 copy-start.31
  165.6 17.0 copy-start.17
  221.0 31.9 copy-start.28
  253.0 4.5 copy-start.5
  257.4 21.4 copy-start.22
  257.4 21.4 copy-start.24
  278.8 8.2 copy-start.29
  278.8 8.2 copy-start.8
  278.9 8.2 copy-start.18
  345.6 18.3 copy-start.9
  648.2 24.3 copy-start.26
  672.5 8.8 copy-start.13
  777.1 552.6 %all-to-all-start = ((bf16[8,1536,2048]{2,1,0:T(8,128)(2,1)}), bf16[8,1536,2048]{2,1,0:T(8,128)(2,1)}, u32[]{:S(2)}, u32[]{:S(2)}) async-start(bf16[8,1536,2048]{2,1,0:T(8,128)(2,1)} %bitcast.285), calls=%async_computation | async-start | bytes 100663296 | tf_op jit(solution)/shard_map/all_to_all | solution.py:118
  1921.8 48.0 %copy-start.11 = (s32[12288]{0:T(1024)S(1)}, s32[12288]{0:T(1024)}, u32[]{:S(2)}) copy-start(s32[12288]{0:T(1024)} %fusion.104) | copy-start | bytes 147460
  2256.2 9.1 copy-start.3
  2256.2 10.5 copy-start.14
  2256.2 11.8 copy-start.10
  2256.2 552.9 %all-to-all-start.2 = ((bf16[8,1536,2048]{2,1,0:T(8,128)(2,1)}), bf16[8,1536,2048]{2,1,0:T(8,128)(2,1)}, u32[]{:S(2)}, u32[]{:S(2)}) async-start(bf16[8,1536,2048]{2,1,0:T(8,128)(2,1)} %bitcast.286), calls=%async_computation.2 | async-start | bytes 100663296 | tf_op jit(solution)/shard_map/all_to_all | solution.py:124
  2274.3 99.1 %copy-start.15 = (s32[12288,1]{0,1:T(1,128)S(1)}, s32[12288,1]{0,1:T(1,128)}, u32[]{:S(2)}) copy-start(s32[12288,1]{0,1:T(1,128)} %reshape_reshape.9) | copy-start | bytes 147460
  2274.3 99.1 %copy-start.16 = (s32[12288]{0:T(1024)S(1)}, s32[12288]{0:T(1024)}, u32[]{:S(2)}) copy-start(s32[12288]{0:T(1024)} %get-tuple-element.203) | copy-start | bytes 147460
  2274.3 100.0 %copy-start.4 = (s32[1,4,512,6]{3,2,1,0:T(8,128)S(1)}, s32[1,4,512,6]{3,2,1,0:T(8,128)}, u32[]{:S(2)}) copy-start(s32[1,4,512,6]{3,2,1,0:T(8,128)} %copy-done.2) | copy-start | bytes 147460
  2407.4 401.7 %copy-start.12 = (s32[12288]{0:T(1024)S(1)}, s32[12288]{0:T(1024)}, u32[]{:S(2)}) copy-start(s32[12288]{0:T(1024)} %broadcast_clamp_fusion) | copy-start | bytes 147460
  3095.4 84.5 %copy-start.7 = (f32[2048,6]{1,0:T(8,128)S(1)}, f32[2048,6]{1,0:T(8,128)}, u32[]{:S(2)}) copy-start(f32[2048,6]{1,0:T(8,128)} %and_select_fusion) | copy-start | bytes 147460
  3179.9 69.6 %copy-start.6 = (bf16[1,4,512,2048]{3,2,1,0:T(8,128)(2,1)S(1)}, bf16[1,4,512,2048]{3,2,1,0:T(8,128)(2,1)}, u32[]{:S(2)}) copy-start(bf16[1,4,512,2048]{3,2,1,0:T(8,128)(2,1)} %get-tuple-element.219) | copy-start | bytes 25165828
  3179.9 69.6 %copy-start.20 = (pred[1,4,4,128]{3,1,2,0:T(4,128)(4,1)S(1)}, pred[1,4,4,128]{3,1,2,0:T(4,128)(4,1)}, u32[]{:S(2)}) copy-start(pred[1,4,4,128]{3,1,2,0:T(4,128)(4,1)} %copy-done.19) | copy-start | bytes 6148
  3249.5 34.2 %copy-start.1 = (bf16[512,16,128]{2,1,0:T(8,128)(2,1)S(1)}, bf16[512,16,128]{2,1,0:T(8,128)(2,1)}, u32[]{:S(2)}) copy-start(bf16[512,16,128]{2,1,0:T(8,128)(2,1)} %param.35) | copy-start | bytes 6291460
where the time goes:
time: 3330 us; the launch traced here: 3280 us
  local copies, waits for them, and re-layouts  1350 us (41%)
  waiting for transfers between devices  804 us (24%)
  matrix products  459 us (14%)
  other arithmetic  384 us (12%)
  Pallas kernels  253 us (8%)
    all_to_all x1, waiting for transfers between devices, device_step(): recv_rows = lax.all_to_all(send_rows, 'dpa', 0, 0, tiled=True)  437 us
    all_to_all x1, waiting for transfers between devices, device_step(): back_rows = lax.all_to_all(expert_rows, 'dpa', 0, 0, tiled=True)  367 us
    gather x1, local copies, waits for them, and re-layouts, device_step(): recv_rows[order]  286 us
    gather x1, local copies, waits for them, and re-layouts, device_step(): expert_rows = sorted_out[jnp.argsort(order)]  286 us
    gather x1, local copies, waits for them, and re-layouts, device_step(): pair_out = back_rows[slot].reshape(tokens, top_k, width)  286 us
    another operation x3, Pallas kernels  251 us
    gather x1, local copies, waits for them, and re-layouts, device_step(): send_key = expert_key[pair_of_slot]  120 us
    sub x4, matrix products, one_request(): attn_prob = jax.nn.softmax(scores, axis=-1).astype(jnp.bfloat16)  104 us
  transfers between devices with their start and end apart: 3, of which 2 were waited for; matrix products, arithmetic and copies ran while one was open for 27% of the time, Pallas kernels for 0%

commit v1 on v0

v1 whole, which is shorter than its diff:
```python
import functools

import jax
import jax.numpy as jnp
from jax import lax
from jax.experimental import pallas as pl
from jax.experimental.pallas import tpu as pltpu
from jax.sharding import PartitionSpec as P

EPS = 1e-6
THETA = 10000.0
NEG = -1e30
UNIT = 16
PIECE = 256
KBLK = 256
TBLK = 128
VMEM = pltpu.VMEM
SMEM = pltpu.SMEM
ANY = pl.ANY
F32 = jnp.float32
BF16 = jnp.bfloat16


def rms_norm(vals, gain):
    vals_f32 = vals.astype(F32)
    inv_rms = lax.rsqrt(jnp.mean(vals_f32 * vals_f32, axis=-1, keepdims=True) + EPS)
    return (vals_f32 * inv_rms * gain.astype(F32)).astype(BF16)


def dot(lhs, rhs):
    return jnp.dot(lhs, rhs, preferred_element_type=F32)


def whole_spec(shape):
    return pl.BlockSpec(shape, lambda *_: (0,) * len(shape), pipeline_mode=pl.Buffered(1))


def attention_kernel(lens, x_ref, a_ref, q_ref, wuk_ref, wuv_ref, wdkv_ref, wkr_ref, cos_ref, sin_ref, perm_ref, gkv_ref, gffn_ref, wo_ref, lat_ref, rope_ref, h_ref, u_ref, lat_out, rope_out, keys_ref, o_ref, *, heads_step, row_blk, key_blk, scale, nope, rope):
    step = pl.program_id(0)
    count, ctx = lens[0], lens[1]
    chunk, width = x_ref.shape
    rank = lat_ref.shape[1]
    ctx_max = lat_ref.shape[0]

    @pl.when(step == 0)
    def _():
        a_val = a_ref[...]
        lat_f32 = dot(a_val, wdkv_ref[...])
        inv_rms = lax.rsqrt(jnp.mean(lat_f32 * lat_f32, axis=-1, keepdims=True) + EPS)
        lat_new = (lat_f32 * inv_rms * gkv_ref[...].astype(F32)).astype(BF16)
        both = dot(a_val, wkr_ref[...])
        rope_new = (both[:, :rope] * cos_ref[...] + both[:, rope:] * sin_ref[...]).astype(BF16)
        for base in range(0, ctx_max, key_blk):
            pos = lax.broadcasted_iota(jnp.int32, (key_blk, chunk), 0) + base - ctx
            row = lax.broadcasted_iota(jnp.int32, (key_blk, chunk), 1)
            pick = ((pos == row) & (row < count)).astype(F32).astype(BF16)
            at = lax.broadcasted_iota(jnp.int32, (key_blk, 1), 0) + base - ctx
            fresh = (at >= 0) & (at < count)
            rows = pl.ds(base, key_blk)
            lat_blk = jnp.where(fresh, dot(pick, lat_new), lat_ref[rows, :].astype(F32))
            rope_blk = jnp.where(fresh, dot(pick, rope_new), rope_ref[rows, :].astype(F32))
            lat_out[rows, :] = lat_blk.astype(BF16)
            rope_out[rows, :] = rope_blk.astype(BF16)
            keys_ref[0:rank, base:base + key_blk] = lat_blk.T.astype(BF16)
            keys_ref[rank:rank + rope, base:base + key_blk] = rope_blk.T.astype(BF16)

    vdim = wuv_ref.shape[2]
    for row0 in range(0, chunk, row_blk):
        rows = slice(row0, row0 + row_blk)
        seen = ctx + jnp.minimum(count, row0 + row_blk)
        blocks = (seen + key_blk - 1) // key_blk
        for n_keys in range(1, ctx_max // key_blk + 1):
            @pl.when((row0 < count) & (blocks == n_keys))
            def _():
                span = n_keys * key_blk
                col = lax.broadcasted_iota(jnp.int32, (row_blk, span), 1)
                row = lax.broadcasted_iota(jnp.int32, (row_blk, span), 0)
                visible = col - row <= ctx + row0
                for sub in range(heads_step):
                    q_val = q_ref[sub, rows, :]
                    q_lat = dot(q_val[:, :nope], wuk_ref[sub]).astype(BF16)
                    q_raw = q_val[:, nope:nope + rope]
                    q_rot = (q_raw.astype(F32) * cos_ref[rows, :] + dot(q_raw, perm_ref[...]) * sin_ref[rows, :]).astype(BF16)
                    scores = (dot(q_lat, keys_ref[0:rank, :span]) + dot(q_rot, keys_ref[rank:rank + rope, :span])) * scale
                    scores = jnp.where(visible, scores, NEG)
                    top = jnp.max(scores, axis=1, keepdims=True)
                    expo = jnp.exp(scores - top)
                    prob = (expo * (1.0 / jnp.sum(expo, axis=1, keepdims=True))).astype(BF16)
                    out_lat = dot(prob, lat_out[0:span, :]).astype(BF16)
                    head = step * heads_step + sub
                    o_ref[rows, pl.ds(pl.multiple_of(head * vdim, vdim), vdim)] = dot(out_lat, wuv_ref[sub]).astype(BF16)

    @pl.when(step == pl.num_programs(0) - 1)
    def _():
        for row0 in range(0, chunk, row_blk):
            rows = slice(row0, row0 + row_blk)

            @pl.when(row0 < count)
            def _():
                def column(index, carry):
                    cols = pl.ds(pl.multiple_of(index * 512, 512), 512)
                    attn = dot(o_ref[rows, :], wo_ref[:, cols]).astype(BF16)
                    h_ref[rows, cols] = (x_ref[rows, cols].astype(F32) + attn.astype(F32)).astype(BF16)
                    return carry

                lax.fori_loop(0, width // 512, column, 0)
                u_ref[rows, :] = rms_norm(h_ref[rows, :], gffn_ref[...])

            @pl.when(row0 >= count)
            def _():
                h_ref[rows, :] = jnp.zeros((row_blk, width), BF16)
                u_ref[rows, :] = jnp.zeros((row_blk, width), BF16)


def attention(req, lens, x_all, a_req, q_req, wuk, wuv, wdkv, wkr2, cos_tab, sin_tab, perm, gkv, gffn, wo, lat_all, rope_all):
    n_req, chunk, width = x_all.shape
    heads, _, qdim = q_req.shape
    rope = perm.shape[0]
    nope = qdim - rope
    _, ctx_max, rank = lat_all.shape
    vdim = wuv.shape[2]
    hstep = 2
    kernel = functools.partial(attention_kernel, heads_step=hstep, row_blk=256, key_blk=256, scale=qdim ** -0.5, nope=nope, rope=rope)

    def one(shape):
        return pl.BlockSpec((None,) + shape, lambda *_: (req,) + (0,) * len(shape), pipeline_mode=pl.Buffered(1))

    def per_head(shape):
        return pl.BlockSpec((hstep,) + shape, lambda i, *_: (i, 0, 0))

    return pl.pallas_call(
        kernel,
        grid_spec=pltpu.PrefetchScalarGridSpec(
            num_scalar_prefetch=1,
            grid=(heads // hstep,),
            in_specs=[
                one((chunk, width)),
                whole_spec((chunk, width)),
                per_head((chunk, qdim)),
                per_head((nope, rank)),
                per_head((rank, vdim)),
                whole_spec(wdkv.shape),
                whole_spec(wkr2.shape),
                one((chunk, rope)),
                one((chunk, rope)),
                whole_spec(perm.shape),
                whole_spec(gkv.shape),
                whole_spec(gffn.shape),
                whole_spec(wo.shape),
                one((ctx_max, rank)),
                one((ctx_max, rope)),
            ],
            out_specs=[
                whole_spec((chunk, width)),
                whole_spec((chunk, width)),
                one((ctx_max, rank)),
                one((ctx_max, rope)),
            ],
            scratch_shapes=[VMEM((rank + rope, ctx_max), BF16), VMEM((chunk, heads * vdim), BF16)],
        ),
        out_shape=[
            jax.ShapeDtypeStruct((chunk, width), BF16),
            jax.ShapeDtypeStruct((chunk, width), BF16),
            jax.ShapeDtypeStruct(lat_all.shape, BF16),
            jax.ShapeDtypeStruct(rope_all.shape, BF16),
        ],
        input_output_aliases={14: 2, 15: 3},
        compiler_params=pltpu.CompilerParams(vmem_limit_bytes=58 << 20),
        cost_estimate=pl.CostEstimate(flops=30 * 10 ** 9, bytes_accessed=24 << 20, transcendentals=chunk * heads * ctx_max // 2),
        name=f"attention_{req}",
    )(lens, x_all, a_req, q_req, wuk, wuv, wdkv, wkr2, cos_tab, sin_tab, perm, gkv, gffn, wo, lat_all, rope_all)


def slot_table(topk, valid, n_exp, group):
    tokens, top_k = topk.shape
    local = n_exp // group
    ids = jnp.arange(n_exp, dtype=jnp.int32)
    hit = jnp.any(topk.T[:, None, :] == ids[None, :, None], axis=0) & valid[None, :]
    incl = jnp.cumsum(hit.astype(jnp.int32), axis=1)
    before = incl - hit.astype(jnp.int32)
    units = (incl[:, -1] + UNIT - 1) // UNIT
    turn = (before // UNIT).reshape(group, local, tokens)
    rank = jnp.zeros_like(turn)
    own = jnp.arange(local, dtype=jnp.int32)[None, :, None]
    per = units.reshape(group, local)
    for other in range(local):
        have = per[:, other][:, None, None]
        rank = rank + jnp.minimum(have, turn) + ((own > other) & (have > turn)).astype(jnp.int32)
    slot = rank.reshape(n_exp, tokens) * UNIT + before % UNIT
    return jnp.where(hit, slot, -1), jnp.sum(per, axis=1)


def owner_tables(slots, n_pieces):
    group, local, tokens = slots.shape
    per = PIECE // UNIT
    units = (jnp.sum((slots >= 0).astype(jnp.int32), axis=2) + UNIT - 1) // UNIT
    cap = n_pieces * per
    turn = jnp.arange(tokens // UNIT, dtype=jnp.int32)[None, None, :]
    rank = jnp.zeros((group, local, tokens // UNIT), jnp.int32)
    own = jnp.arange(local, dtype=jnp.int32)[None, :, None]
    for other in range(local):
        have = units[:, other][:, None, None]
        rank = rank + jnp.minimum(have, turn) + ((own > other) & (have > turn)).astype(jnp.int32)
    rank = jnp.where(turn < units[:, :, None], rank, -1)
    expert = jnp.max(jnp.where(rank[:, None, :, :] == jnp.arange(cap, dtype=jnp.int32)[None, :, None, None], own[:, None], -1), axis=(2, 3))
    expert = jnp.where(expert < 0, local, expert).reshape(group, n_pieces, per).transpose(1, 0, 2).reshape(n_pieces, group * per)
    order = jnp.arange(group * per, dtype=jnp.int32)
    key = expert * (group * per) + order
    pos = jnp.sum((key[:, None, :] < key[:, :, None]).astype(jnp.int32), axis=2)
    inv = jnp.sum(jnp.where(pos[:, None, :] == order[None, :, None], order[None, None, :], 0), axis=2)
    first = jnp.sum((expert[:, None, :] < jnp.arange(local + 1, dtype=jnp.int32)[None, :, None]).astype(jnp.int32), axis=2)
    n_blk = tokens // KBLK
    piece = jnp.where(slots >= 0, slots // PIECE, -1).reshape(group, local, n_blk, KBLK)
    active = jnp.any(piece[None] == jnp.arange(n_pieces, dtype=jnp.int32)[:, None, None, None, None], axis=(2, 4)).reshape(n_pieces, group * n_blk)
    items, n_items = compact(active)
    return pos, inv, first, items, n_items


def compact(active):
    size = active.shape[-1]
    ids = jnp.arange(size, dtype=jnp.int32)
    flag = active.astype(jnp.int32)
    place = jnp.sum(jnp.where(ids[None, :] < ids[:, None], flag[:, None, :], 0), axis=2)
    items = jnp.sum(jnp.where((place[:, None, :] == ids[None, :, None]) & active[:, None, :], ids[None, None, :], 0), axis=2)
    return items, jnp.sum(flag, axis=1)


def expert_kernel(n_src, pos_ref, inv_ref, first_ref, item_ref, count_ref, slot_ref, *refs, n_req, piece):
    u_refs = refs[:n_req]
    wg_hbm, wu_hbm, wd_hbm, out_hbm, trash, wgu, wdn, rows_ref, acc, ubuf, obuf, zbuf, wsem, usem, osem, zsem = refs[n_req:]
    local = wg_hbm.shape[0]
    ff = wg_hbm.shape[2]
    per = piece // UNIT
    tile = obuf.shape[1]
    tile_units = tile // UNIT
    n_blk = slot_ref.shape[1] // KBLK
    req_blk = n_blk // n_req
    n_items = count_ref[0]
    depth = ubuf.shape[0]
    base = count_ref[1]

    def weights(exp, slot):
        return (
            pltpu.make_async_copy(wg_hbm.at[exp], wgu.at[slot, :, pl.ds(0, ff)], wsem.at[slot, 0]),
            pltpu.make_async_copy(wu_hbm.at[exp], wgu.at[slot, :, pl.ds(ff, ff)], wsem.at[slot, 1]),
            pltpu.make_async_copy(wd_hbm.at[exp], wdn.at[slot], wsem.at[slot, 2]),
        )

    def token_copy(ref, src, blk, slot):
        start = pl.multiple_of((src * req_blk + blk % req_blk) * KBLK, KBLK)
        return pltpu.make_async_copy(ref.at[pl.ds(start, KBLK), :], ubuf.at[slot], usem.at[slot])

    def fetch(index):
        item = item_ref[index]
        src, blk = item // n_blk, item % n_blk
        for req in range(n_req):
            @pl.when(blk // req_blk == req)
            def _():
                token_copy(u_refs[req], src, blk, index % depth).start()

    @pl.when(n_items > 0)
    def _():
        for copy in weights(0, 0):
            copy.start()
        for index in range(depth - 1):
            @pl.when(index < n_items)
            def _():
                fetch(index)

    zbuf[...] = jnp.zeros_like(zbuf)
    used = first_ref[local]

    def unit_rows(unit):
        return pl.ds(pl.multiple_of(unit * UNIT, UNIT), UNIT)

    def blank(index, carry):
        pltpu.make_async_copy(zbuf, out_hbm.at[unit_rows(inv_ref[index])], zsem).start()
        return carry

    lax.fori_loop(used, n_src * per, blank, 0)

    def gather(index, carry):
        item = item_ref[index]
        src, blk = item // n_blk, item % n_blk
        slot = index % depth
        token_copy(u_refs[0], 0, 0, slot).wait()

        @pl.when(index + depth - 1 < n_items)
        def _():
            fetch(index + depth - 1)

        at = slot_ref[pl.ds(pl.multiple_of(src * local, local), local), pl.ds(pl.multiple_of(blk * KBLK, KBLK), KBLK)] - base
        row = lax.broadcasted_iota(jnp.int32, (piece, KBLK), 0)
        pick = at[0:1, :] == row
        for exp in range(1, local):
            pick = pick | (at[exp:exp + 1, :] == row)
        part = dot(pick.astype(F32).astype(BF16), ubuf[slot])
        prev = item_ref[jnp.maximum(index - 1, 0)] // n_blk
        after = item_ref[jnp.minimum(index + 1, n_items - 1)] // n_blk
        opens = (index == 0) | (prev != src)
        closes = (index == n_items - 1) | (after != src)

        @pl.when(opens)
        def _():
            acc[...] = part

        @pl.when(jnp.logical_not(opens))
        def _():
            acc[...] += part

        @pl.when(closes)
        def _():
            for unit in range(per):
                rows_ref[unit_rows(pos_ref[src * per + unit]), :] = acc[unit * UNIT:(unit + 1) * UNIT, :].astype(BF16)

        return carry

    lax.fori_loop(0, n_items, gather, 0)

    def store(slot):
        return pltpu.make_async_copy(obuf.at[slot], trash.at[slot], osem.at[slot])

    def expert(exp, done):
        slot = exp % 2
        for copy in weights(exp, slot):
            copy.wait()

        @pl.when(exp + 1 < local)
        def _():
            for copy in weights(exp + 1, 1 - slot):
                copy.start()

        begin, end = first_ref[exp], first_ref[exp + 1]

        def one_tile(index, done):
            unit0 = begin + index * tile_units
            x_val = rows_ref[pl.ds(pl.multiple_of(unit0 * UNIT, UNIT), tile), :]
            hid = dot(x_val, wgu[slot])
            gate = hid[:, :ff]
            act = (gate * jax.nn.sigmoid(gate) * hid[:, ff:]).astype(BF16)
            side = done % 2

            @pl.when(done >= 2)
            def _():
                store(side).wait()

            obuf[side] = dot(act, wdn[slot]).astype(BF16)
            for unit in range(tile_units):
                src = obuf.at[side, pl.ds(unit * UNIT, UNIT), :]

                @pl.when(unit0 + unit < end)
                def _():
                    pltpu.make_async_copy(src, out_hbm.at[unit_rows(inv_ref[jnp.minimum(unit0 + unit, n_src * per - 1)])], osem.at[side]).start()

                @pl.when(unit0 + unit >= end)
                def _():
                    pltpu.make_async_copy(src, trash.at[side, pl.ds(unit * UNIT, UNIT), :], osem.at[side]).start()

            return done + 1

        return lax.fori_loop(0, (end - begin + tile_units - 1) // tile_units, one_tile, done)

    n_exp = jnp.where(n_items > 0, local, 0)
    done = lax.fori_loop(0, n_exp, expert, 0)

    def drain(side):
        @pl.when(done > side)
        def _():
            store(side).wait()

    drain(0)
    drain(1)

    def blank_wait(index, carry):
        pltpu.make_async_copy(zbuf, out_hbm.at[pl.ds(0, UNIT), :], zsem).wait()
        return carry

    lax.fori_loop(used, n_src * per, blank_wait, 0)


def experts(index, tables, slots, gathered, w_gate, w_up, w_down):
    pos, inv, first, items, n_items = tables
    group, local, tokens = slots.shape
    n_req = len(gathered)
    _, width, ff = w_gate.shape
    tile = 256
    rows = group * PIECE
    info = jnp.stack([n_items[index], jnp.int32(index * PIECE)])
    kernel = functools.partial(expert_kernel, group, n_req=n_req, piece=PIECE)
    out, _ = pl.pallas_call(
        kernel,
        grid_spec=pltpu.PrefetchScalarGridSpec(
            num_scalar_prefetch=5,
            grid=(1,),
            in_specs=[whole_spec((group * local, tokens))] + [pl.BlockSpec(memory_space=ANY)] * (n_req + 3),
            out_specs=[pl.BlockSpec(memory_space=ANY)] * 2,
            scratch_shapes=[
                VMEM((2, width, 2 * ff), BF16),
                VMEM((2, ff, width), BF16),
                VMEM((rows + tile, width), BF16),
                VMEM((PIECE, width), F32),
                VMEM((3, KBLK, width), BF16),
                VMEM((2, tile, width), BF16),
                VMEM((UNIT, width), BF16),
                pltpu.SemaphoreType.DMA((2, 3)),
                pltpu.SemaphoreType.DMA((3,)),
                pltpu.SemaphoreType.DMA((2,)),
                pltpu.SemaphoreType.DMA,
            ],
        ),
        out_shape=[jax.ShapeDtypeStruct((rows, width), BF16), jax.ShapeDtypeStruct((2, tile, width), BF16)],
        compiler_params=pltpu.CompilerParams(vmem_limit_bytes=62 << 20),
        cost_estimate=pl.CostEstimate(flops=6 * rows * width * ff, bytes_accessed=6 * local * width * ff, transcendentals=rows * ff),
        name=f"experts_{index}",
    )(pos[index], inv[index], first[index], items[index], info, slots.reshape(group * local, tokens), *gathered, w_gate, w_up, w_down)
    return out.reshape(group, PIECE, width)


def sum_kernel(item_ref, count_ref, len_ref, slot_ref, prob_ref, back_ref, *refs, n_req, piece):
    accs = refs[n_req + 1:2 * n_req + 1]
    y_hbm, gates, abuf, ybuf, isem, osem, ysem = refs[2 * n_req + 1:]
    group = back_ref.shape[0] // piece
    local = slot_ref.shape[0] // group
    base = count_ref[1]
    n_items = count_ref[0]
    req_blk = slot_ref.shape[1] // TBLK // n_req
    chunk = req_blk * TBLK

    def each(blk, todo):
        for req in range(n_req):
            @pl.when(blk // req_blk == req)
            def _():
                todo(accs[req].at[pl.ds(pl.multiple_of((blk % req_blk) * TBLK, TBLK), TBLK), :])

    def load(index):
        side = index % 2
        each(item_ref[index], lambda ref: pltpu.make_async_copy(ref, abuf.at[side], isem.at[side]).start())

    def save_wait(side):
        pltpu.make_async_copy(abuf.at[side], accs[0].at[pl.ds(0, TBLK), :], osem.at[side]).wait()
        pltpu.make_async_copy(ybuf.at[side], y_hbm.at[pl.ds(0, TBLK), :], ysem.at[side]).wait()

    @pl.when(n_items > 0)
    def _():
        load(0)

    def body(index, carry):
        blk = item_ref[index]
        side = index % 2
        cols = pl.ds(pl.multiple_of(blk * TBLK, TBLK), TBLK)
        row = lax.broadcasted_iota(jnp.int32, (piece, TBLK), 0)
        for owner in range(group):
            at = slot_ref[owner * local:(owner + 1) * local, cols] - base
            prob = prob_ref[owner * local:(owner + 1) * local, cols]
            gate = jnp.zeros((piece, TBLK), F32)
            for exp in range(local):
                gate = jnp.where(at[exp:exp + 1, :] == row, prob[exp:exp + 1, :], gate)
            high = gate.astype(BF16)
            rest = gate - high.astype(F32)
            mid = rest.astype(BF16)
            low = (rest - mid.astype(F32)).astype(BF16)
            rows = slice(owner * piece, (owner + 1) * piece)
            gates[rows, 0:TBLK] = high
            gates[rows, TBLK:2 * TBLK] = mid
            gates[rows, 2 * TBLK:3 * TBLK] = low
        pltpu.make_async_copy(accs[0].at[pl.ds(0, TBLK), :], abuf.at[side], isem.at[side]).wait()

        @pl.when(index >= 1)
        def _():
            save_wait(1 - side)

        @pl.when(index + 1 < n_items)
        def _():
            load(index + 1)

        req = blk // req_blk
        keep = len_ref[req] - (blk % req_blk) * TBLK
        good = lax.broadcasted_iota(jnp.int32, (TBLK, 1), 0) < keep
        width = abuf.shape[2]
        step = 512

        def column(part, carry):
            at = pl.ds(pl.multiple_of(part * step, step), step)
            out = lax.dot_general(gates[...], back_ref[:, at], (((0,), (0,)), ((), ())), preferred_element_type=F32)
            total = abuf[side, :, at] + (out[0:TBLK] + (out[TBLK:2 * TBLK] + out[2 * TBLK:]))
            abuf[side, :, at] = total
            ybuf[side, :, at] = jnp.where(good, total, 0.0).astype(BF16)
            return carry

        lax.fori_loop(0, width // step, column, 0)
        each(blk, lambda ref: pltpu.make_async_copy(abuf.at[side], ref, osem.at[side]).start())
        pltpu.make_async_copy(ybuf.at[side], y_hbm.at[cols, :], ysem.at[side]).start()
        return carry

    lax.fori_loop(0, n_items, body, 0)

    @pl.when(n_items > 0)
    def _():
        save_wait((n_items - 1) % 2)


def sum_piece(index, home, lens, slot, prob, back, accs, y_buf):
    items, n_items = home
    n_exp, tokens = slot.shape
    group, piece, width = back.shape
    n_req = len(accs)
    info = jnp.stack([n_items[index], jnp.int32(index * PIECE)])
    outs = pl.pallas_call(
        functools.partial(sum_kernel, n_req=n_req, piece=piece),
        grid_spec=pltpu.PrefetchScalarGridSpec(
            num_scalar_prefetch=3,
            grid=(1,),
            in_specs=[whole_spec((n_exp, tokens)), whole_spec((n_exp, tokens)), whole_spec((group * piece, width))] + [pl.BlockSpec(memory_space=ANY)] * (n_req + 1),
            out_specs=[pl.BlockSpec(memory_space=ANY)] * (n_req + 1),
            scratch_shapes=[
                VMEM((group * piece, 3 * TBLK), BF16),
                VMEM((2, TBLK, width), F32),
                VMEM((2, TBLK, width), BF16),
                pltpu.SemaphoreType.DMA((2,)),
                pltpu.SemaphoreType.DMA((2,)),
                pltpu.SemaphoreType.DMA((2,)),
            ],
        ),
        out_shape=[jax.ShapeDtypeStruct(acc.shape, F32) for acc in accs] + [jax.ShapeDtypeStruct(y_buf.shape, BF16)],
        input_output_aliases={6 + i: i for i in range(n_req + 1)},
        compiler_params=pltpu.CompilerParams(vmem_limit_bytes=40 << 20),
        cost_estimate=pl.CostEstimate(flops=2 * 3 * 512 * group * piece * width, bytes_accessed=16 << 20, transcendentals=0),
        name=f"sum_{index}",
    )(items[index], info, lens, slot, prob, back.reshape(group * piece, width), *accs, y_buf)
    return outs[:n_req], outs[n_req]


def solution(mesh):
    group = mesh.shape['dpa']
    tok_spec = P(('dp', 'dpa'))
    whole = P()
    exp_spec = P('dpa')

    def device_step(x_in, chunk_len, ctx_len, lat_cache, rope_cache, topk_idx, g_attn, w_q, w_dkv, g_kv, w_kr, w_uk, w_uv, w_o, g_ffn, w_router, w_sh_gate, w_sh_up, w_sh_down, w_exp_gate, w_exp_up, w_exp_down):
        _, n_req, chunk, width = x_in.shape
        rope = w_kr.shape[1]
        half = rope // 2
        heads, vdim = w_o.shape[:2]
        tokens = n_req * chunk
        top_k = topk_idx.shape[-1]
        n_exp = w_router.shape[1]
        local = n_exp // group
        capacity = tokens * top_k // group
        cap_units = capacity // UNIT + local
        n_pieces = -(-cap_units * UNIT // PIECE)
        lens, ctx = chunk_len[0], ctx_len[0]
        x_all = x_in[0]

        valid = (jnp.arange(chunk)[None, :] < lens[:, None]).reshape(tokens)
        slot, n_units = slot_table(topk_idx.reshape(tokens, top_k), valid, n_exp, group)
        slots = lax.all_to_all(slot.reshape(group, local, tokens), 'dpa', 0, 0, tiled=True)
        tables = owner_tables(slots, n_pieces)
        own_piece = jnp.where(slot >= 0, slot // PIECE, -1).reshape(n_exp, tokens // TBLK, TBLK)
        home = compact(jnp.any(own_piece[None] == jnp.arange(n_pieces, dtype=jnp.int32)[:, None, None, None], axis=(1, 3)))

        inv_freq = THETA ** (-2.0 * jnp.arange(half, dtype=F32) / rope)
        angle = (ctx[:, None] + jnp.arange(chunk)).astype(F32)[..., None] * inv_freq
        cos_tab = jnp.concatenate([jnp.cos(angle), jnp.cos(angle)], axis=-1)
        sin_tab = jnp.concatenate([-jnp.sin(angle), jnp.sin(angle)], axis=-1)
        perm = jnp.roll(jnp.eye(rope, dtype=F32), half, axis=1).astype(BF16)
        wkr2 = jnp.concatenate([w_kr, w_kr[:, half:], w_kr[:, :half]], axis=1)
        wuk = w_uk.transpose(1, 2, 0)
        wuv = w_uv.transpose(1, 0, 2)
        wo = w_o.reshape(heads * vdim, width)
        lat_all, rope_all = lat_cache[0], rope_cache[0]
        gathered, accs, probs = [], [], []
        for req in range(n_req):
            a_req = rms_norm(x_all[req], g_attn)
            q_req = jnp.einsum('cd,dhq->hcq', a_req, w_q, preferred_element_type=F32).astype(BF16)
            h_req, u_req, lat_all, rope_all = attention(req, jnp.stack([lens[req], ctx[req]]), x_all, a_req, q_req, wuk, wuv, w_dkv, wkr2, cos_tab, sin_tab, perm, g_kv[None], g_ffn[None], wo, lat_all, rope_all)
            gathered.append(lax.all_gather(u_req, 'dpa', axis=0, tiled=True))
            probs.append(jax.nn.softmax(dot(u_req, w_router), axis=-1).T)
            act = (jax.nn.silu(dot(u_req, w_sh_gate)) * dot(u_req, w_sh_up)).astype(BF16)
            accs.append(h_req.astype(F32) + dot(act, w_sh_down))
        prob = jnp.concatenate(probs, axis=1)

        y_buf = jnp.zeros((tokens, width), BF16)
        for index in range(n_pieces):
            sent = experts(index, tables, slots, gathered, w_exp_gate, w_exp_up, w_exp_down)
            back = lax.all_to_all(sent, 'dpa', 0, 0, tiled=True)
            accs, y_buf = sum_piece(index, home, lens, slot, prob, back, accs, y_buf)
        return y_buf.reshape(x_in.shape), lat_all[None], rope_all[None]

    return jax.shard_map(device_step, mesh=mesh, in_specs=(tok_spec,) * 6 + (whole,) * 13 + (exp_spec,) * 3, out_specs=(tok_spec, tok_spec, tok_spec), check_vma=False)
```

time: 3330 us -> 1440 us (0.43)
  local copies, waits for them, and re-layouts: 1350 us -> 64.6 us
  waiting for transfers between devices: 804 us -> 98.8 us
  Pallas kernels: 253 us -> 910 us
  other arithmetic: 384 us -> 88.1 us
  matrix products: 459 us -> 194 us
    gather x32 -> x0, local copies, waits for them, and re-layouts: 1200 us -> none  [the longest x1 286 us: device_step(): recv_rows[order]]
    pallas_call x0 -> x18, Pallas kernels: none -> 910 us  [the longest x7 446 us: experts(): pl.pallas_call(kernel, grid_spec=pltpu.PrefetchScalarGridSpec(num_scalar_...]
    all_to_all x3 -> x8, waiting for transfers between devices: 804 us -> 75.9 us  [the longest x7 75.9 us: device_step(): back = lax.all_to_all(sent, 'dpa', 0, 0, tiled=True)]
    another operation x3 -> x0, Pallas kernels: 251 us -> none
    dot_general x18 -> x12, matrix products: 354 us -> 156 us  [dot(): return jnp.dot(lhs, rhs, preferred_element_type=F32)]
    convert_element_type x9 -> x10, other arithmetic: 117 us -> 7.86 us  [the longest x2 5.98 us: rms_norm(): return (vals_f32 * inv_rms * gain.astype(F32)).astype(BF16)]
    sub x4 -> x0, matrix products: 104 us -> none  [one_request(): attn_prob = jax.nn.softmax(scores, axis=-1).astype(jnp.bfloat16)]
    scatter-add x1 -> x0, other arithmetic: 85.8 us -> none  [device_step(): jnp.bincount(recv_key, length=local_exp + 1)[:local_exp].astype(jnp.int32)]
  transfers between devices with their start and end apart: 3 -> 12, of which waited for: 2 -> 3; matrix products, arithmetic and copies ran while one was open for 27% -> 20% of each run, Pallas kernels for 0% -> 54%
where the time goes in v1:
time: 1440 us; the launch traced here: 1420 us
  Pallas kernels  910 us (63%)
  matrix products  194 us (13%)
  waiting for transfers between devices  98.8 us (7%)
  other arithmetic  88.1 us (6%)
  local copies, waits for them, and re-layouts  64.6 us (4%)
  starting transfers between devices  51.8 us (4%)
  between operations  15.5 us (1%)
    pallas_call x7, Pallas kernels, experts(): pl.pallas_call(kernel, grid_spec=pltpu.PrefetchScalarGridSpec(num_scalar_...  446 us
    pallas_call x4, Pallas kernels, attention(): pl.pallas_call(kernel, grid_spec=pltpu.PrefetchScalarGridSpec(num_scalar_...  254 us
    pallas_call x7, Pallas kernels, sum_piece(): pl.pallas_call(functools.partial(sum_kernel, n_req=n_req, piece=piece), g...  209 us
    dot_general x12, matrix products, dot(): return jnp.dot(lhs, rhs, preferred_element_type=F32)  156 us
    all_to_all x7, waiting for transfers between devices, device_step(): back = lax.all_to_all(sent, 'dpa', 0, 0, tiled=True)  75.9 us
    all_to_all x7, starting transfers between devices, device_step(): back = lax.all_to_all(sent, 'dpa', 0, 0, tiled=True)  39.3 us
    unnamed x4, matrix products  38.1 us
    unnamed x174, local copies, waits for them, and re-layouts  31.8 us
  transfers between devices with their start and end apart: 12, of which 3 were waited for; matrix products, arithmetic and copies ran while one was open for 20% of the time, Pallas kernels for 54%

profile of v1, /device:TPU:112, one launch (start us, length us, event | category | flops | bytes accessed | tf_op | source)
XLA Modules:
  0.0 1422.2 jit_solution(2053214595887272837)
XLA Ops:
  7.3 4.8 copy.195
  26.9 6.0 fusion.2
  32.8 10.1 fusion.59
  43.4 3.9 copy.127
  58.2 60.4 %attention_0.1 = (bf16[512,2048]{1,0:T(8,128)(2,1)}, bf16[512,2048]{1,0:T(8,128)(2,1)}, bf16[4,1024,512]{2,1,0:T(8,128)(2,1)}, bf16[4,1024,64]{2,1,0:T(8,128)(2,1)}) custom-call(s32[2]{0:T(128)} %pad_add_fusion.14.lens, bf16[4,512,2048]{2,1,0:T(8,128)(2,1)} %bitcast.215, ...), custom_call_target="tpu_custom_call", output_to_operand_aliasing={{2}: (14, {}), {3}: (15, {})} | custom-call | flops 30000001024 | bytes 25165824 | tf_op jit(solution)/shard_map/attention_0/pallas_call | solution.py:131
  118.7 9.3 fusion.60
  128.5 3.9 copy.134
  134.2 60.4 %attention_1.1 = (bf16[512,2048]{1,0:T(8,128)(2,1)}, bf16[512,2048]{1,0:T(8,128)(2,1)}, bf16[4,1024,512]{2,1,0:T(8,128)(2,1)}, bf16[4,1024,64]{2,1,0:T(8,128)(2,1)}) custom-call(s32[2]{0:T(128)} %pad_add_fusion.15.lens, bf16[4,512,2048]{2,1,0:T(8,128)(2,1)} %bitcast.216, ...), custom_call_target="tpu_custom_call", output_to_operand_aliasing={{2}: (14, {}), {3}: (15, {})} | custom-call | flops 30000001024 | bytes 25165824 | tf_op jit(solution)/shard_map/attention_1/pallas_call | solution.py:131
  194.8 9.3 fusion.61
  210.4 66.0 %attention_2.1 = (bf16[512,2048]{1,0:T(8,128)(2,1)}, bf16[512,2048]{1,0:T(8,128)(2,1)}, bf16[4,1024,512]{2,1,0:T(8,128)(2,1)}, bf16[4,1024,64]{2,1,0:T(8,128)(2,1)}) custom-call(s32[2]{0:T(128)} %pad_add_fusion.16.lens, bf16[4,512,2048]{2,1,0:T(8,128)(2,1)} %bitcast.217, ...), custom_call_target="tpu_custom_call", output_to_operand_aliasing={{2}: (14, {}), {3}: (15, {})} | custom-call | flops 30000001024 | bytes 25165824 | tf_op jit(solution)/shard_map/attention_2/pallas_call | solution.py:131
  276.6 9.3 fusion.62
  292.1 67.4 %attention_3.1 = (bf16[512,2048]{1,0:T(8,128)(2,1)}, bf16[512,2048]{1,0:T(8,128)(2,1)}, bf16[4,1024,512]{2,1,0:T(8,128)(2,1)}, bf16[4,1024,64]{2,1,0:T(8,128)(2,1)}) custom-call(s32[2]{0:T(128)} %pad_add_fusion.17.lens, bf16[4,512,2048]{2,1,0:T(8,128)(2,1)} %bitcast.218, ...), custom_call_target="tpu_custom_call", output_to_operand_aliasing={{2}: (14, {}), {3}: (15, {})} | custom-call | flops 30000001024 | bytes 25165824 | tf_op jit(solution)/shard_map/attention_3/pallas_call | solution.py:131
  360.6 18.1 %reduce-window.6 = s32[64,16,128]{2,1,0:T(8,128)S(1)} reduce-window(s32[64,16,128]{2,1,0:T(8,128)S(1)} %fusion.30, s32[]{:T(128)} %constant.120.clone.1), window={size=1x1x128 pad=0_0x0_0x127_0}, to_apply=%region_1.0 | reduce-window | flops 16646144 | bytes 1048580 | tf_op jit(solution)/shard_map/reduce-window
  383.1 12.3 all-to-all-start
  421.4 16.4 %select_reduce_fusion = s32[8,112]{1,0:T(8,128)S(1)} fusion(s32[8,8,128]{2,1,0:T(8,128)S(1)} %add_select_fusion.8), kind=kLoop, calls=%fused_computation.29 | loop fusion | flops 2751616 | bytes 36352 | tf_op jit(solution)/shard_map/reduce_max | solution.py:205
  444.1 22.7 %all-gather.11.cloned.1.call-done.refs_3_ = bf16[4096,2048]{1,0:T(8,128)(2,1)} async-done(((bf16[512,2048]{1,0:T(8,128)(2,1)}), bf16[4096,2048]{1,0:T(8,128)(2,1)}) %all-gather.11.cloned.1.call-update) | async-done | bytes 16777232 | tf_op jit(solution)/shard_map/all_gather | solution.py:576
  466.8 73.6 %experts_0.1 = (bf16[2048,2048]{1,0:T(8,128)(2,1)}, bf16[2,256,2048]{2,1,0:T(8,128)(2,1)}) custom-call(s32[128]{0:T(128)} %get-tuple-element.180.pos_ref, s32[128]{0:T(128)} %get-tuple-element.173.inv_ref, s32[9]{0:T(128)} %get-tuple-element.130.first_ref, s32[64]{0:T(128)} %get-tuple-element.166.item_ref, s32[2]{0:T(128)} %pad_add_fusion.12.count_ref, ...), custom_call_target="tpu_custom_call" | custom-call | flops 35433480192 | bytes 138412032 | tf_op jit(solution)/shard_map/experts_0/pallas_call | solution.py:390
  540.4 5.3 all-to-all-start.7
  545.9 12.6 fusion.63
  558.5 11.1 fusion.64
  570.8 79.3 %experts_1.1 = (bf16[2048,2048]{1,0:T(8,128)(2,1)}, bf16[2,256,2048]{2,1,0:T(8,128)(2,1)}) custom-call(s32[128]{0:T(128)} %get-tuple-element.181.pos_ref, s32[128]{0:T(128)} %get-tuple-element.174.inv_ref, s32[9]{0:T(128)} %get-tuple-element.131.first_ref, s32[64]{0:T(128)} %get-tuple-element.167.item_ref, s32[2]{0:T(128)} %pad_add_fusion.10.count_ref, ...), custom_call_target="tpu_custom_call" | custom-call | flops 35433480192 | bytes 138412032 | tf_op jit(solution)/shard_map/experts_1/pallas_call | solution.py:390
  650.3 6.1 all-to-all-start.6
  658.4 12.6 fusion.65
  671.1 11.1 fusion.66
  683.4 81.3 %experts_2.1 = (bf16[2048,2048]{1,0:T(8,128)(2,1)}, bf16[2,256,2048]{2,1,0:T(8,128)(2,1)}) custom-call(s32[128]{0:T(128)} %get-tuple-element.182.pos_ref, s32[128]{0:T(128)} %get-tuple-element.175.inv_ref, s32[9]{0:T(128)} %get-tuple-element.132.first_ref, s32[64]{0:T(128)} %get-tuple-element.168.item_ref, s32[2]{0:T(128)} %pad_add_fusion.8.count_ref, ...), custom_call_target="tpu_custom_call" | custom-call | flops 35433480192 | bytes 138412032 | tf_op jit(solution)/shard_map/experts_2/pallas_call | solution.py:390
  764.8 7.3 all-to-all-start.5
  772.1 24.6 %convert_add_fusion.3.refs_0_ = f32[512,2048]{1,0:T(8,128)} fusion(bf16[512,2048]{1,0:T(8,128)(2,1)} %get-tuple-element.74, bf16[2816,2048]{1,0:T(8,128)(2,1)} %param.40, f32[512,2816]{1,0:T(8,128)} %fusion.63, bf16[512,2048]{1,0:T(8,128)(2,1)} %get-tuple-element.57, bf16[2048,2816]{1,0:T(8,128)(2,1)} %param.39), kind=kOutput, calls=%fused_computation.27 | convolution fusion | flops 11821907968 | bytes 37224448 | tf_op jit(solution)/shard_map/dot_general | solution.py:31
  797.9 81.0 %experts_3.1 = (bf16[2048,2048]{1,0:T(8,128)(2,1)}, bf16[2,256,2048]{2,1,0:T(8,128)(2,1)}) custom-call(s32[128]{0:T(128)} %get-tuple-element.183.pos_ref, s32[128]{0:T(128)} %get-tuple-element.176.inv_ref, s32[9]{0:T(128)} %get-tuple-element.133.first_ref, s32[64]{0:T(128)} %get-tuple-element.169.item_ref, s32[2]{0:T(128)} %pad_add_fusion.6.count_ref, ...), custom_call_target="tpu_custom_call" | custom-call | flops 35433480192 | bytes 138412032 | tf_op jit(solution)/shard_map/experts_3/pallas_call | solution.py:390
  878.9 5.2 all-to-all-start.4
  884.1 24.6 %convert_add_fusion.2.refs_1_ = f32[512,2048]{1,0:T(8,128)} fusion(bf16[512,2048]{1,0:T(8,128)(2,1)} %get-tuple-element.75, bf16[2816,2048]{1,0:T(8,128)(2,1)} %param.40, f32[512,2816]{1,0:T(8,128)} %fusion.64, bf16[512,2048]{1,0:T(8,128)(2,1)} %get-tuple-element.60, bf16[2048,2816]{1,0:T(8,128)(2,1)} %param.39), kind=kOutput, calls=%fused_computation.26 | convolution fusion | flops 11821907968 | bytes 37224448 | tf_op jit(solution)/shard_map/dot_general | solution.py:31
  910.0 70.1 %experts_4.1 = (bf16[2048,2048]{1,0:T(8,128)(2,1)}, bf16[2,256,2048]{2,1,0:T(8,128)(2,1)}) custom-call(s32[128]{0:T(128)} %get-tuple-element.184.pos_ref, s32[128]{0:T(128)} %get-tuple-element.177.inv_ref, s32[9]{0:T(128)} %get-tuple-element.134.first_ref, s32[64]{0:T(128)} %get-tuple-element.170.item_ref, s32[2]{0:T(128)} %pad_add_fusion.4.count_ref, ...), custom_call_target="tpu_custom_call" | custom-call | flops 35433480192 | bytes 138412032 | tf_op jit(solution)/shard_map/experts_4/pallas_call | solution.py:390
  980.1 5.1 all-to-all-start.3
  985.2 24.7 %convert_add_fusion.1.refs_2_ = f32[512,2048]{1,0:T(8,128)} fusion(bf16[512,2048]{1,0:T(8,128)(2,1)} %get-tuple-element.76, bf16[2816,2048]{1,0:T(8,128)(2,1)} %param.40, f32[512,2816]{1,0:T(8,128)} %fusion.65, bf16[512,2048]{1,0:T(8,128)(2,1)} %get-tuple-element.63, bf16[2048,2816]{1,0:T(8,128)(2,1)} %param.39), kind=kOutput, calls=%fused_computation.25 | convolution fusion | flops 11821907968 | bytes 37224448 | tf_op jit(solution)/shard_map/dot_general | solution.py:31
  1011.1 55.9 %experts_5.1 = (bf16[2048,2048]{1,0:T(8,128)(2,1)}, bf16[2,256,2048]{2,1,0:T(8,128)(2,1)}) custom-call(s32[128]{0:T(128)} %get-tuple-element.185.pos_ref, s32[128]{0:T(128)} %get-tuple-element.178.inv_ref, s32[9]{0:T(128)} %get-tuple-element.135.first_ref, s32[64]{0:T(128)} %get-tuple-element.171.item_ref, s32[2]{0:T(128)} %pad_add_fusion.2.count_ref, ...), custom_call_target="tpu_custom_call" | custom-call | flops 35433480192 | bytes 138412032 | tf_op jit(solution)/shard_map/experts_5/pallas_call | solution.py:390
  1067.0 12.6 all-to-all-done.3
  1079.6 5.1 all-to-all-start.2
  1084.7 24.8 %convert_add_fusion.refs_3_ = f32[512,2048]{1,0:T(8,128)} fusion(bf16[512,2048]{1,0:T(8,128)(2,1)} %get-tuple-element.77, bf16[2816,2048]{1,0:T(8,128)(2,1)} %param.40, f32[512,2816]{1,0:T(8,128)} %fusion.66, bf16[512,2048]{1,0:T(8,128)(2,1)} %get-tuple-element.66, bf16[2048,2816]{1,0:T(8,128)(2,1)} %param.39), kind=kOutput, calls=%fused_computation.24 | convolution fusion | flops 11821907968 | bytes 37224448 | tf_op jit(solution)/shard_map/dot_general | solution.py:31
  1110.6 5.1 experts_6.1
  1115.8 63.3 %all-to-all-done.2 = bf16[8,256,2048]{2,1,0:T(8,128)(2,1)} async-done(((bf16[8,256,2048]{2,1,0:T(8,128)(2,1)}), bf16[8,256,2048]{2,1,0:T(8,128)(2,1)}, u32[]{:S(2)}, u32[]{:S(2)}) %all-to-all-start.2) | async-done | bytes 8388640 | tf_op jit(solution)/shard_map/all_to_all | solution.py:585
  1179.1 5.1 all-to-all-start.1
  1185.0 5.3 broadcast_in_dim.115.refs_4_
  1193.7 26.2 %sum_0.1 = (f32[512,2048]{1,0:T(8,128)S(1)}, f32[512,2048]{1,0:T(8,128)S(1)}, f32[512,2048]{1,0:T(8,128)S(1)}, f32[512,2048]{1,0:T(8,128)}, bf16[2048,2048]{1,0:T(8,128)(2,1)}) custom-call(s32[16]{0:T(128)S(1)} %get-tuple-element.187.item_ref, ...), custom_call_target="tpu_custom_call", output_to_operand_aliasing={{0}: (6, {}), {1}: (7, {}), {2}: (8, {}), {3}: (9, {}), {4}... | custom-call | flops 12884901888 | bytes 16777216 | tf_op jit(solution)/shard_map/sum_0/pallas_call | solution.py:508
  1219.9 36.9 %sum_1.1 = (f32[512,2048]{1,0:T(8,128)S(1)}, f32[512,2048]{1,0:T(8,128)S(1)}, f32[512,2048]{1,0:T(8,128)S(1)}, f32[512,2048]{1,0:T(8,128)}, bf16[2048,2048]{1,0:T(8,128)(2,1)}) custom-call(s32[16]{0:T(128)S(1)} %get-tuple-element.188.item_ref, ...), custom_call_target="tpu_custom_call", output_to_operand_aliasing={{0}: (6, {}), {1}: (7, {}), {2}: (8, {}), {3}: (9, {}), {4}... | custom-call | flops 12884901888 | bytes 16777216 | tf_op jit(solution)/shard_map/sum_1/pallas_call | solution.py:508
  1256.9 36.9 %sum_2.1 = (f32[512,2048]{1,0:T(8,128)S(1)}, f32[512,2048]{1,0:T(8,128)S(1)}, f32[512,2048]{1,0:T(8,128)S(1)}, f32[512,2048]{1,0:T(8,128)}, bf16[2048,2048]{1,0:T(8,128)(2,1)}) custom-call(s32[16]{0:T(128)S(1)} %get-tuple-element.189.item_ref, ...), custom_call_target="tpu_custom_call", output_to_operand_aliasing={{0}: (6, {}), {1}: (7, {}), {2}: (8, {}), {3}: (9, {}), {4}... | custom-call | flops 12884901888 | bytes 16777216 | tf_op jit(solution)/shard_map/sum_2/pallas_call | solution.py:508
  1293.8 47.8 %sum_3.1 = (f32[512,2048]{1,0:T(8,128)S(1)}, f32[512,2048]{1,0:T(8,128)S(1)}, f32[512,2048]{1,0:T(8,128)S(1)}, f32[512,2048]{1,0:T(8,128)}, bf16[2048,2048]{1,0:T(8,128)(2,1)}) custom-call(s32[16]{0:T(128)S(1)} %get-tuple-element.190.item_ref, ...), custom_call_target="tpu_custom_call", output_to_operand_aliasing={{0}: (6, {}), {1}: (7, {}), {2}: (8, {}), {3}: (9, {}), {4}... | custom-call | flops 12884901888 | bytes 16777216 | tf_op jit(solution)/shard_map/sum_3/pallas_call | solution.py:508
  1341.5 36.7 %sum_4.1 = (f32[512,2048]{1,0:T(8,128)S(1)}, f32[512,2048]{1,0:T(8,128)S(1)}, f32[512,2048]{1,0:T(8,128)S(1)}, f32[512,2048]{1,0:T(8,128)}, bf16[2048,2048]{1,0:T(8,128)(2,1)}) custom-call(s32[16]{0:T(128)S(1)} %get-tuple-element.191.item_ref, ...), custom_call_target="tpu_custom_call", output_to_operand_aliasing={{0}: (6, {}), {1}: (7, {}), {2}: (8, {}), {3}: (9, {}), {4}... | custom-call | flops 12884901888 | bytes 16777216 | tf_op jit(solution)/shard_map/sum_4/pallas_call | solution.py:508
  1378.2 20.8 %sum_5.1 = (f32[512,2048]{1,0:T(8,128)S(1)}, f32[512,2048]{1,0:T(8,128)S(1)}, f32[512,2048]{1,0:T(8,128)S(1)}, f32[512,2048]{1,0:T(8,128)}, bf16[2048,2048]{1,0:T(8,128)(2,1)}) custom-call(s32[16]{0:T(128)S(1)} %get-tuple-element.192.item_ref, ...), custom_call_target="tpu_custom_call", output_to_operand_aliasing={{0}: (6, {}), {1}: (7, {}), {2}: (8, {}), {3}: (9, {}), {4}... | custom-call | flops 12884901888 | bytes 16777216 | tf_op jit(solution)/shard_map/sum_5/pallas_call | solution.py:508
  1411.4 4.0 sum_6.1
  (349 shorter events, 104.1 us)
Async XLA Ops:
  7.2 398.5 %copy-start = (bf16[2048,64]{0,1:T(8,128)(2,1)S(1)}, bf16[2048,64]{0,1:T(8,128)(2,1)}, u32[]{:S(2)}) copy-start(bf16[2048,64]{0,1:T(8,128)(2,1)} %param.37) | copy-start | bytes 786436
  7.2 436.8 %all-gather.5.cloned.1.call-start = ((), (), s32[]{:S(2)}) async-start(), calls=%async_computation.8 | async-start | bytes 18874368 | tf_op jit(solution)/shard_map/all_gather | solution.py:576
  58.2 60.5 %copy-start.24 = (bf16[512,2048]{1,0:T(8,128)(2,1)S(1)}, bf16[512,2048]{1,0:T(8,128)(2,1)}, u32[]{:S(2)}) copy-start(bf16[512,2048]{1,0:T(8,128)(2,1)} %get-tuple-element.154.a_ref) | copy-start | bytes 6291460
  118.6 325.5 %all-gather.7.cloned.1.call-start = ((), (), s32[]{:S(2)}) async-start(), calls=%async_computation.9 | async-start | bytes 18874368 | tf_op jit(solution)/shard_map/all_gather | solution.py:576
  134.2 60.6 %copy-start.23 = (bf16[512,2048]{1,0:T(8,128)(2,1)S(1)}, bf16[512,2048]{1,0:T(8,128)(2,1)}, u32[]{:S(2)}) copy-start(bf16[512,2048]{1,0:T(8,128)(2,1)} %get-tuple-element.155.a_ref) | copy-start | bytes 6291460
  194.7 249.4 %all-gather.9.cloned.1.call-start = ((), (), s32[]{:S(2)}) async-start(), calls=%async_computation.10 | async-start | bytes 18874368 | tf_op jit(solution)/shard_map/all_gather | solution.py:576
  210.4 66.2 %copy-start.22 = (bf16[512,2048]{1,0:T(8,128)(2,1)S(1)}, bf16[512,2048]{1,0:T(8,128)(2,1)}, u32[]{:S(2)}) copy-start(bf16[512,2048]{1,0:T(8,128)(2,1)} %get-tuple-element.156.a_ref) | copy-start | bytes 6291460
  276.5 190.3 %all-gather.11.cloned.1.call-start = ((), (), s32[]{:S(2)}) async-start(), calls=%async_computation.11 | async-start | bytes 18874368 | tf_op jit(solution)/shard_map/all_gather | solution.py:576
  292.1 67.5 %copy-start.3 = (s32[1,4]{1,0:T(1,128)S(1)}, s32[1,4]{1,0:T(1,128)}, u32[]{:S(2)}) copy-start(s32[1,4]{1,0:T(1,128)} %param.23) | copy-start | bytes 52
  292.1 67.8 %copy-start.34 = (s32[1,4,512,6]{2,1,3,0:T(4,128)S(1)}, s32[1,4,512,6]{2,1,3,0:T(4,128)}, u32[]{:S(2)}) copy-start(s32[1,4,512,6]{2,1,3,0:T(4,128)} %param.27) | copy-start | bytes 147460
  359.7 23.4 %copy-start.35 = (pred[1,4,4,128]{3,1,2,0:T(4,128)(4,1)}, pred[1,4,4,128]{3,1,2,0:T(4,128)(4,1)S(1)}, u32[]{:S(2)}) copy-start(pred[1,4,4,128]{3,1,2,0:T(4,128)(4,1)S(1)} %copy.144) | copy-start | bytes 6148
  360.4 22.7 %copy-start.26 = (pred[64,2048]{1,0:T(8,128)(4,1)}, pred[64,2048]{1,0:T(8,128)(4,1)S(1)}, u32[]{:S(2)}) copy-start(pred[64,2048]{1,0:T(8,128)(4,1)S(1)} %fusion.14) | copy-start | bytes 393220
  379.8 28.2 %copy-start.18 = (s32[64,16,128]{2,1,0:T(8,128)}, s32[64,16,128]{2,1,0:T(8,128)S(1)}, u32[]{:S(2)}) copy-start(s32[64,16,128]{2,1,0:T(8,128)S(1)} %broadcast_add_fusion) | copy-start | bytes 1572868
  380.4 17.0 %copy-start.73 = (pred[8]{0:T(512)(128)(4,1)}, pred[8]{0:T(512)(128)(4,1)S(1)}, u32[]{:S(2)}) copy-start(pred[8]{0:T(512)(128)(4,1)S(1)} %get-tuple-element.226) | copy-start | bytes 28
  380.4 17.0 %copy-start.75 = (pred[8]{0:T(512)(128)(4,1)}, pred[8]{0:T(512)(128)(4,1)S(1)}, u32[]{:S(2)}) copy-start(pred[8]{0:T(512)(128)(4,1)S(1)} %get-tuple-element.227) | copy-start | bytes 28
  380.4 17.0 %copy-start.77 = (pred[8]{0:T(512)(128)(4,1)}, pred[8]{0:T(512)(128)(4,1)S(1)}, u32[]{:S(2)}) copy-start(pred[8]{0:T(512)(128)(4,1)S(1)} %get-tuple-element.224) | copy-start | bytes 28
  380.4 17.0 %copy-start.79 = (pred[8]{0:T(512)(128)(4,1)}, pred[8]{0:T(512)(128)(4,1)S(1)}, u32[]{:S(2)}) copy-start(pred[8]{0:T(512)(128)(4,1)S(1)} %get-tuple-element.225) | copy-start | bytes 28
  383.1 34.9 %all-to-all-start = ((s32[8,8,2048]{2,1,0:T(8,128)}), s32[8,8,2048]{2,1,0:T(8,128)S(1)}, u32[]{:S(2)}, u32[]{:S(2)}) async-start(s32[8,8,2048]{2,1,0:T(8,128)} %fusion.22), calls=%async_computation | async-start | bytes 1048576 | tf_op jit(solution)/shard_map/all_to_all | solution.py:556
  395.4 17.5 %copy-start.57 = (pred[64]{0:T(512)(128)(4,1)}, pred[64]{0:T(512)(128)(4,1)S(1)}, u32[]{:S(2)}) copy-start(pred[64]{0:T(512)(128)(4,1)S(1)} %and.509) | copy-start | bytes 196
  395.5 17.4 %copy-start.59 = (pred[64]{0:T(512)(128)(4,1)}, pred[64]{0:T(512)(128)(4,1)S(1)}, u32[]{:S(2)}) copy-start(pred[64]{0:T(512)(128)(4,1)S(1)} %and.505) | copy-start | bytes 196
  395.6 17.3 %copy-start.61 = (pred[64]{0:T(512)(128)(4,1)}, pred[64]{0:T(512)(128)(4,1)S(1)}, u32[]{:S(2)}) copy-start(pred[64]{0:T(512)(128)(4,1)S(1)} %and.517) | copy-start | bytes 196
  395.8 17.2 %copy-start.63 = (pred[64]{0:T(512)(128)(4,1)}, pred[64]{0:T(512)(128)(4,1)S(1)}, u32[]{:S(2)}) copy-start(pred[64]{0:T(512)(128)(4,1)S(1)} %and.513) | copy-start | bytes 196
  395.9 17.1 %copy-start.65 = (pred[64]{0:T(512)(128)(4,1)}, pred[64]{0:T(512)(128)(4,1)S(1)}, u32[]{:S(2)}) copy-start(pred[64]{0:T(512)(128)(4,1)S(1)} %and.525) | copy-start | bytes 196
  396.0 17.0 %copy-start.67 = (pred[64]{0:T(512)(128)(4,1)}, pred[64]{0:T(512)(128)(4,1)S(1)}, u32[]{:S(2)}) copy-start(pred[64]{0:T(512)(128)(4,1)S(1)} %and.521) | copy-start | bytes 196
  396.1 16.9 %copy-start.69 = (pred[64]{0:T(512)(128)(4,1)}, pred[64]{0:T(512)(128)(4,1)S(1)}, u32[]{:S(2)}) copy-start(pred[64]{0:T(512)(128)(4,1)S(1)} %and.533) | copy-start | bytes 196
  396.2 16.8 %copy-start.71 = (pred[64]{0:T(512)(128)(4,1)}, pred[64]{0:T(512)(128)(4,1)S(1)}, u32[]{:S(2)}) copy-start(pred[64]{0:T(512)(128)(4,1)S(1)} %and.529) | copy-start | bytes 196
  396.3 16.7 %copy-start.39 = (s32[64]{0:T(128)}, s32[64]{0:T(128)S(1)}, u32[]{:S(2)}) copy-start(s32[64]{0:T(128)S(1)} %min.402) | copy-start | bytes 772
  396.5 16.5 %copy-start.41 = (s32[64]{0:T(128)}, s32[64]{0:T(128)S(1)}, u32[]{:S(2)}) copy-start(s32[64]{0:T(128)S(1)} %min.437) | copy-start | bytes 772
  396.6 16.4 %copy-start.43 = (s32[64]{0:T(128)}, s32[64]{0:T(128)S(1)}, u32[]{:S(2)}) copy-start(s32[64]{0:T(128)S(1)} %min.432) | copy-start | bytes 772
  396.8 16.2 %copy-start.45 = (s32[64]{0:T(128)}, s32[64]{0:T(128)S(1)}, u32[]{:S(2)}) copy-start(s32[64]{0:T(128)S(1)} %min.427) | copy-start | bytes 772
  396.9 16.1 %copy-start.47 = (s32[64]{0:T(128)}, s32[64]{0:T(128)S(1)}, u32[]{:S(2)}) copy-start(s32[64]{0:T(128)S(1)} %min.422) | copy-start | bytes 772
  397.1 15.9 %copy-start.49 = (s32[64]{0:T(128)}, s32[64]{0:T(128)S(1)}, u32[]{:S(2)}) copy-start(s32[64]{0:T(128)S(1)} %min.417) | copy-start | bytes 772
  397.2 15.8 %copy-start.51 = (s32[64]{0:T(128)}, s32[64]{0:T(128)S(1)}, u32[]{:S(2)}) copy-start(s32[64]{0:T(128)S(1)} %min.412) | copy-start | bytes 772
  397.4 15.6 %copy-start.53 = (s32[64]{0:T(128)}, s32[64]{0:T(128)S(1)}, u32[]{:S(2)}) copy-start(s32[64]{0:T(128)S(1)} %min.407) | copy-start | bytes 772
  399.8 14.6 %copy-start.21 = (bf16[4,1024,64]{2,1,0:T(8,128)(2,1)S(1)}, bf16[4,1024,64]{2,1,0:T(8,128)(2,1)}, u32[]{:S(2)}) copy-start(bf16[4,1024,64]{2,1,0:T(8,128)(2,1)} %get-tuple-element.110) | copy-start | bytes 1572868
  410.5 10.7 copy-start.74
  410.5 10.7 copy-start.76
  410.5 10.7 copy-start.78
  418.0 48.8 %copy-start.14 = (s32[8,8,2048]{2,1,0:T(8,128)}, s32[8,8,2048]{2,1,0:T(8,128)S(1)}, u32[]{:S(2)}) copy-start(s32[8,8,2048]{2,1,0:T(8,128)S(1)} %all-to-all-done) | copy-start | bytes 1572868
  540.4 109.7 %all-to-all-start.7 = ((bf16[8,256,2048]{2,1,0:T(8,128)(2,1)}), bf16[8,256,2048]{2,1,0:T(8,128)(2,1)}, u32[]{:S(2)}, u32[]{:S(2)}) async-start(bf16[8,256,2048]{2,1,0:T(8,128)(2,1)} %bitcast.221), calls=%async_computation.7 | async-start | bytes 16777216 | tf_op jit(solution)/shard_map/all_to_all | solution.py:585
  545.9 12.6 copy-start.16
  650.3 114.4 %all-to-all-start.6 = ((bf16[8,256,2048]{2,1,0:T(8,128)(2,1)}), bf16[8,256,2048]{2,1,0:T(8,128)(2,1)}, u32[]{:S(2)}, u32[]{:S(2)}) async-start(bf16[8,256,2048]{2,1,0:T(8,128)(2,1)} %bitcast.220), calls=%async_computation.6 | async-start | bytes 16777216 | tf_op jit(solution)/shard_map/all_to_all | solution.py:585
  658.4 12.6 copy-start.17
  764.8 114.1 %all-to-all-start.5 = ((bf16[8,256,2048]{2,1,0:T(8,128)(2,1)}), bf16[8,256,2048]{2,1,0:T(8,128)(2,1)}, u32[]{:S(2)}, u32[]{:S(2)}) async-start(bf16[8,256,2048]{2,1,0:T(8,128)(2,1)} %bitcast.223), calls=%async_computation.5 | async-start | bytes 16777216 | tf_op jit(solution)/shard_map/all_to_all | solution.py:585
  878.9 101.1 %all-to-all-start.4 = ((bf16[8,256,2048]{2,1,0:T(8,128)(2,1)}), bf16[8,256,2048]{2,1,0:T(8,128)(2,1)}, u32[]{:S(2)}, u32[]{:S(2)}) async-start(bf16[8,256,2048]{2,1,0:T(8,128)(2,1)} %bitcast.224), calls=%async_computation.4 | async-start | bytes 16777216 | tf_op jit(solution)/shard_map/all_to_all | solution.py:585
  980.1 99.5 %all-to-all-start.3 = ((bf16[8,256,2048]{2,1,0:T(8,128)(2,1)}), bf16[8,256,2048]{2,1,0:T(8,128)(2,1)}, u32[]{:S(2)}, u32[]{:S(2)}) async-start(bf16[8,256,2048]{2,1,0:T(8,128)(2,1)} %bitcast.225), calls=%async_computation.3 | async-start | bytes 16777216 | tf_op jit(solution)/shard_map/all_to_all | solution.py:585
  1079.6 99.5 %all-to-all-start.2 = ((bf16[8,256,2048]{2,1,0:T(8,128)(2,1)}), bf16[8,256,2048]{2,1,0:T(8,128)(2,1)}, u32[]{:S(2)}, u32[]{:S(2)}) async-start(bf16[8,256,2048]{2,1,0:T(8,128)(2,1)} %bitcast.222), calls=%async_computation.2 | async-start | bytes 16777216 | tf_op jit(solution)/shard_map/all_to_all | solution.py:585
  1179.1 225.7 %all-to-all-start.1 = ((bf16[8,256,2048]{2,1,0:T(8,128)(2,1)}), bf16[8,256,2048]{2,1,0:T(8,128)(2,1)}, u32[]{:S(2)}, u32[]{:S(2)}) async-start(bf16[8,256,2048]{2,1,0:T(8,128)(2,1)} %bitcast.219), calls=%async_computation.1 | async-start | bytes 16777216 | tf_op jit(solution)/shard_map/all_to_all | solution.py:585
  (46 other events, 251.8 us)
Sparse Core Ops, SparseCore 0:
  118.7 90.9 all-gather.4
  211.3 81.6 all-gather.6
  294.6 81.6 all-gather.8
  377.7 89.0 all-gather.10

commit v2 on v0

v2 whole, which is shorter than its diff:
```python
import functools

import jax
import jax.numpy as jnp
from jax import lax
from jax.experimental import pallas as pl
from jax.experimental.pallas import tpu as pltpu
from jax.sharding import PartitionSpec as P


EPS = 1e-6
THETA = 10000.0
NEG = -1e30
UNIT = 16
PIECE = 256
FIXED = 4
PART = 128
TBLK = 128
TERMS = 3
COLS = 512
GROUP_BLKS = 4
EARLY = 3
N = None
I32 = jnp.int32
FIRST_DIMS = (((0,), (0,)), ((), ()))
LAST_DIMS = (((1,), (1,)), ((), ()))
MIB = 1 << 20
VMEM = pltpu.VMEM
ANY = pl.ANY
F32 = jnp.float32
BF16 = jnp.bfloat16


def rms_norm(vals, gain):
    vals_f32 = vals.astype(F32)
    inv_rms = lax.rsqrt(jnp.mean(vals_f32 * vals_f32, axis=-1, keepdims=True) + EPS)
    return (vals_f32 * inv_rms * gain.astype(F32)).astype(BF16)


def dot(lhs, rhs):
    return jnp.dot(lhs, rhs, preferred_element_type=F32)


def whole_spec(shape):
    return pl.BlockSpec(shape, lambda *_: (0,) * len(shape), pipeline_mode=pl.Buffered(1))


def attention_kernel(info, x_hbm, a_ref, q_ref, wuk_ref, wuv_ref, wdkv_ref, wkr_ref, cos_ref, sin_ref, gkv_ref, gffn_ref, wo_hbm, lat_ref, rope_ref, h_ref, u_ref, lat_out, rope_out, keys_ref, o_ref, xbuf, wo_ref, sems, *, heads_step, row_blk, key_blk, scale, nope):
    step = pl.program_id(0)
    count, ctx, req = (info[i] for i in range(3))
    chunk, width = a_ref.shape
    rank = lat_ref.shape[1]
    ctx_max = lat_ref.shape[0]
    rope = rope_ref.shape[0]
    half = rope // 2
    late = (
        pltpu.make_async_copy(x_hbm.at[req], xbuf, sems.at[0]),
        pltpu.make_async_copy(wo_hbm, wo_ref, sems.at[1]),
    )

    def turned(vals, cols):
        other = jnp.concatenate([vals[half:], vals[:half]], axis=0)
        return (vals * cos_ref[:, cols] + other * sin_ref[:, cols]).astype(BF16)

    @pl.when(step == 0)
    def _():
        for copy in late:
            copy.start()
        a_val = a_ref[...]
        lat_f32 = dot(a_val, wdkv_ref[...])
        inv_rms = lax.rsqrt(jnp.mean(lat_f32 * lat_f32, axis=-1, keepdims=True) + EPS)
        lat_new = (lat_f32 * inv_rms * gkv_ref[...].astype(F32)).astype(BF16)
        rope_new = turned(dot(a_val, wkr_ref[...]).T, slice(None))
        for base in range(0, ctx_max, key_blk):
            rows = pl.ds(base, key_blk)
            touched = (base < ctx + count) & (base + key_blk > ctx)

            @pl.when(touched)
            def _():
                pos = lax.broadcasted_iota(I32, (key_blk, chunk), 0) + base - ctx
                row = lax.broadcasted_iota(I32, (key_blk, chunk), 1)
                pick = (pos == row).astype(F32).astype(BF16)
                at = lax.broadcasted_iota(I32, (key_blk, 1), 0) + base - ctx
                lat_blk = jnp.where((at >= 0) & (at < count), dot(pick, lat_new), lat_ref[rows, :].astype(F32))
                lat_out[rows, :] = lat_blk.astype(BF16)
                keys_ref[0:rank, rows] = lat_blk.T.astype(BF16)
                moved = lax.dot_general(rope_new, pick, LAST_DIMS, preferred_element_type=F32)
                at = lax.broadcasted_iota(I32, (1, key_blk), 1) + base - ctx
                rope_blk = jnp.where((at >= 0) & (at < count), moved, rope_ref[:, rows].astype(F32)).astype(BF16)
                rope_out[:, rows] = rope_blk
                keys_ref[rank:rank + rope, rows] = rope_blk

            @pl.when(jnp.logical_not(touched))
            def _():
                lat_out[rows, :] = lat_ref[rows, :]
                keys_ref[0:rank, rows] = lat_ref[rows, :].astype(F32).T.astype(BF16)
                rope_out[:, rows] = rope_ref[:, rows]
                keys_ref[rank:rank + rope, rows] = rope_ref[:, rows]

    vdim = wuv_ref.shape[2]
    n_rows = (count + row_blk - 1) // row_blk

    def row_block(index, carry):
        row0 = pl.multiple_of(index * row_blk, row_blk)
        rows = pl.ds(row0, row_blk)
        blocks = (ctx + jnp.minimum(count, row0 + row_blk) + key_blk - 1) // key_blk

        def variant(n_keys):
            span = n_keys * key_blk
            col = lax.broadcasted_iota(I32, (row_blk, span), 1)
            row = lax.broadcasted_iota(I32, (row_blk, span), 0)
            visible = col - row <= ctx + row0
            q_lat, q_rot, probs = {}, {}, {}

            def query(sub):
                q_lat[sub] = lax.dot_general(q_ref[sub, 0:nope, rows], wuk_ref[sub], FIRST_DIMS, preferred_element_type=F32).astype(BF16)
                q_rot[sub] = turned(q_ref[sub, nope:nope + rope, rows].astype(F32), rows)

            def score(sub):
                both = dot(q_lat[sub], keys_ref[0:rank, :span]) + lax.dot_general(q_rot[sub], keys_ref[rank:rank + rope, :span], FIRST_DIMS, preferred_element_type=F32)
                probs[sub] = jnp.where(visible, both * scale, NEG)

            def soften(sub):
                expo = jnp.exp(probs[sub] - jnp.max(probs[sub], axis=1, keepdims=True))
                probs[sub] = (expo * (1.0 / jnp.sum(expo, axis=1, keepdims=True))).astype(BF16)

            def finish(sub):
                out_lat = dot(probs[sub], lat_out[0:span, :]).astype(BF16)
                head = step * heads_step + sub
                o_ref[rows, pl.ds(pl.multiple_of(head * vdim, vdim), vdim)] = dot(out_lat, wuv_ref[sub]).astype(BF16)

            for sub in range(heads_step):
                query(sub)
            score(0)
            for sub in range(heads_step):
                if sub + 1 < heads_step:
                    score(sub + 1)
                soften(sub)
                finish(sub)

        most = ctx_max // key_blk
        for n_keys in range(2, most + 1):
            @pl.when((blocks == n_keys) | ((n_keys == 2) & (blocks < 2)))
            def _():
                variant(n_keys)

        return carry

    lax.fori_loop(0, n_rows, row_block, 0)

    @pl.when(step == pl.num_programs(0) - 1)
    def _():
        for copy in late:
            copy.wait()

        def project(index, carry):
            rows = pl.ds(pl.multiple_of(index * row_blk, row_blk), row_blk)

            def column(part, carry):
                cols = pl.ds(pl.multiple_of(part * 512, 512), 512)
                attn = dot(o_ref[rows, :], wo_ref[:, cols]).astype(BF16)
                h_ref[rows, cols] = (xbuf[rows, cols].astype(F32) + attn.astype(F32)).astype(BF16)
                return carry

            lax.fori_loop(0, width // 512, column, 0)
            u_ref[rows, :] = rms_norm(h_ref[rows, :], gffn_ref[...])
            return carry

        def blank(index, carry):
            rows = pl.ds(pl.multiple_of(index * row_blk, row_blk), row_blk)
            h_ref[rows, :] = jnp.zeros((row_blk, width), BF16)
            u_ref[rows, :] = jnp.zeros((row_blk, width), BF16)
            return carry

        lax.fori_loop(0, n_rows, project, 0)
        lax.fori_loop(n_rows, chunk // row_blk, blank, 0)


def attention(info, x_all, a_req, q_req, wuk, wuv, wdkv, wkr, cos_tab, sin_tab, gkv, gffn, wo, lat_all, rope_all):
    _, chunk, width = x_all.shape
    heads, qdim, _ = q_req.shape
    rope = wkr.shape[1]
    nope = qdim - rope
    _, ctx_max, rank = lat_all.shape
    vdim = wuv.shape[2]
    hstep = 4
    kernel = functools.partial(attention_kernel, heads_step=hstep, row_blk=256, key_blk=256, scale=qdim ** -0.5, nope=nope)

    def one(shape):
        return pl.BlockSpec((N,) + shape, lambda _, info: (info[2],) + (0,) * len(shape), pipeline_mode=pl.Buffered(1))

    def per_head(shape):
        return pl.BlockSpec((hstep,) + shape, lambda i, *_: (i, 0, 0))

    return pl.pallas_call(
        kernel,
        grid_spec=pltpu.PrefetchScalarGridSpec(
            num_scalar_prefetch=1,
            grid=(heads // hstep,),
            in_specs=[
                pl.BlockSpec(memory_space=ANY),
                whole_spec((chunk, width)),
                per_head((qdim, chunk)),
                per_head((nope, rank)),
                per_head((rank, vdim)),
                whole_spec(wdkv.shape),
                whole_spec(wkr.shape),
                one((rope, chunk)),
                one((rope, chunk)),
                whole_spec(gkv.shape),
                whole_spec(gffn.shape),
                pl.BlockSpec(memory_space=ANY),
                one((ctx_max, rank)),
                one((rope, ctx_max)),
            ],
            out_specs=[
                whole_spec((chunk, width)),
                whole_spec((chunk, width)),
                one((ctx_max, rank)),
                one((rope, ctx_max)),
            ],
            scratch_shapes=[
                VMEM((rank + rope, ctx_max), BF16),
                VMEM((chunk, heads * vdim), BF16),
                VMEM((chunk, width), BF16),
                VMEM(wo.shape, BF16),
                pltpu.SemaphoreType.DMA((2,)),
            ],
        ),
        out_shape=[
            jax.ShapeDtypeStruct((chunk, width), BF16),
            jax.ShapeDtypeStruct((chunk, width), BF16),
            jax.ShapeDtypeStruct(lat_all.shape, BF16),
            jax.ShapeDtypeStruct(rope_all.shape, BF16),
        ],
        input_output_aliases={13: 2, 14: 3},
        compiler_params=pltpu.CompilerParams(vmem_limit_bytes=58 * MIB),
        cost_estimate=pl.CostEstimate(flops=chunk * heads * ctx_max * rank * 4, bytes_accessed=24 * MIB, transcendentals=chunk * heads * ctx_max // 2),
    )(info, x_all, a_req, q_req, wuk, wuv, wdkv, wkr, cos_tab, sin_tab, gkv, gffn, wo, lat_all, rope_all)


def shared_kernel(lens, u_ref, h_ref, wr_ref, wg_hbm, wu_hbm, wd_hbm, total_ref, prob_ref, wg, wu, wd, act, sems):
    index = pl.program_id(0)
    blk, width = u_ref.shape
    ff = act.shape[1]
    step = ff // 2
    copies = [pltpu.make_async_copy(*pair, sems.at[i]) for i, pair in enumerate(((wg_hbm, wg), (wu_hbm, wu), (wd_hbm, wd)))]

    @pl.when(index == 0)
    def _():
        for copy in copies:
            copy.start()

    def wait(some):
        @pl.when(index == 0)
        def _():
            for copy in some:
                copy.wait()

    @pl.when((index * blk < lens[0]) | (index == 0))
    def _():
        logits = lax.dot_general(wr_ref[...], u_ref[...], LAST_DIMS, preferred_element_type=F32)
        expo = jnp.exp(logits - jnp.max(logits, axis=0, keepdims=True))
        prob_ref[...] = expo / jnp.sum(expo, axis=0, keepdims=True)
        wait(copies[:2])
        for part in range(2):
            cols = slice(part * step, (part + 1) * step)
            gate = dot(u_ref[...], wg[:, cols])
            act[:, cols] = (gate * jax.nn.sigmoid(gate) * dot(u_ref[...], wu[:, cols])).astype(BF16)
        wait(copies[2:])
        for start in range(0, width, COLS):
            cols = slice(start, start + COLS)
            total_ref[:, cols] = h_ref[:, cols].astype(F32) + dot(act[...], wd[:, cols])


def shared(count, u_req, h_req, w_router, w_gate, w_up, w_down):
    chunk, width = u_req.shape
    ff = w_gate.shape[1]
    n_exp = w_router.shape[1]
    blk = PIECE
    rows = pl.BlockSpec((blk, width), lambda i, *_: (i, 0))
    return pl.pallas_call(
        shared_kernel,
        grid_spec=pltpu.PrefetchScalarGridSpec(
            num_scalar_prefetch=1,
            grid=(chunk // blk,),
            in_specs=[rows, rows, whole_spec((n_exp, width))] + [pl.BlockSpec(memory_space=ANY)] * 3,
            out_specs=[rows, pl.BlockSpec((n_exp, blk), lambda i, *_: (0, i))],
            scratch_shapes=[VMEM(w_gate.shape, BF16), VMEM(w_up.shape, BF16), VMEM(w_down.shape, BF16), VMEM((blk, ff), BF16), pltpu.SemaphoreType.DMA((3,))],
        ),
        out_shape=[jax.ShapeDtypeStruct((chunk, width), F32), jax.ShapeDtypeStruct((n_exp, chunk), F32)],
        compiler_params=pltpu.CompilerParams(vmem_limit_bytes=62 * MIB),
        cost_estimate=pl.CostEstimate(flops=6 * chunk * width * ff, bytes_accessed=6 * width * ff, transcendentals=chunk * ff),
    )(count, u_req, h_req, w_router.T, w_gate, w_up, w_down)


def unit_ranks(units, turn):
    local = units.shape[-1]
    own = jnp.arange(local, dtype=I32)[:, N]
    rank = jnp.zeros_like(turn)
    for other in range(local):
        have = units[..., other][..., None, None]
        rank = rank + jnp.minimum(have, turn) + ((own > other) & (have > turn)).astype(I32)
    return rank


def slot_table(topk, valid, n_exp, group):
    tokens = topk.shape[0]
    local = n_exp // group
    ids = jnp.arange(n_exp, dtype=I32)
    hit = jnp.any(topk.T[:, None, :] == ids[None, :, None], axis=0) & valid[N, :]
    ones = hit.astype(BF16).reshape(n_exp, tokens // 128, 128)
    low = (jnp.arange(128)[:, N] < jnp.arange(128)[N, :]).astype(BF16)
    inner = jnp.einsum('ebt,ts->ebs', ones, low, preferred_element_type=F32)
    sums = jnp.sum(ones.astype(F32), axis=2)
    n_blk = tokens // 128
    outer = jnp.einsum('eb,bc->ec', sums.astype(BF16), (jnp.arange(n_blk)[:, N] < jnp.arange(n_blk)[N, :]).astype(BF16), preferred_element_type=F32)
    before = (inner + outer[:, :, None]).astype(I32).reshape(group, local, tokens)
    units = (jnp.sum(sums, axis=1).astype(I32).reshape(group, local) + UNIT - 1) // UNIT
    slot = unit_ranks(units, before // UNIT) * UNIT + before % UNIT
    return jnp.where(hit, slot.reshape(n_exp, tokens), -1), jnp.sum(units, axis=1)


def compact(active):
    size = active.shape[-1]
    ids = jnp.arange(size, dtype=I32)
    flag = active.astype(I32)
    place = jnp.sum(jnp.where(ids[N, :] < ids[:, N], flag[..., None, :], 0), axis=-1)
    items = jnp.sum(jnp.where((place[..., None, :] == ids[:, N]) & active[..., None, :], ids, 0), axis=-1)
    return items, jnp.sum(flag, axis=-1)


def piece_of(slot, starts):
    return sum((slot >= first).astype(I32) for first in starts) - 1


def owner_tables(slots, starts, sizes):
    group, local, tokens = slots.shape
    n_pieces = len(starts)
    per = max(sizes) // UNIT
    units = (jnp.sum((slots >= 0).astype(I32), axis=2) + UNIT - 1) // UNIT
    places = jnp.arange(per, dtype=I32)
    ranks = jnp.array(starts, I32)[:, N] // UNIT + places
    real = places < jnp.array(sizes, I32)[:, N] // UNIT
    flat = ranks.reshape(-1)
    turns = jnp.arange(tokens // UNIT + 1, dtype=I32)
    until = jnp.sum(jnp.minimum(units[:, :, N], turns), axis=1)
    turn = jnp.sum((until[:, N, 1:] <= flat[:, N]).astype(I32), axis=2)
    start = jnp.sum(jnp.minimum(units[:, N, :], turn[:, :, N]), axis=2)
    has = units[:, N, :] > turn[:, :, N]
    upto = jnp.sum((has[:, :, N, :] & (jnp.arange(local)[N, :] <= jnp.arange(local)[:, N])).astype(I32), axis=3)
    expert = jnp.sum((upto <= (flat - start)[:, :, N]).astype(I32), axis=2).reshape(group, n_pieces, per)
    expert = jnp.where(real, expert, local + 1).transpose(1, 0, 2).reshape(n_pieces, group * per)
    order = jnp.arange(group * per, dtype=I32)
    key = expert * (group * per) + order
    pos = jnp.sum((key[:, N, :] < key[:, :, N]).astype(I32), axis=2)
    inv = jnp.sum(jnp.where(pos[:, N, :] == order[:, N], order, 0), axis=2)
    first = jnp.sum((expert[:, N, :] < jnp.arange(local + 2, dtype=I32)[:, N]).astype(I32), axis=2)
    n_blk = tokens // TBLK
    piece = piece_of(slots, starts).reshape(group, local, n_blk, TBLK)
    active = jnp.any(piece == jnp.arange(n_pieces, dtype=I32)[:, N, N, N, N], axis=(2, 4))
    blocks, n_blocks = compact(active)
    groups = jnp.arange(n_blk // GROUP_BLKS, dtype=I32) * GROUP_BLKS
    items, n_items = compact((n_blocks[:, :, N] > groups).reshape(n_pieces, group * (n_blk // GROUP_BLKS)))
    return pos, inv, first, blocks.reshape(n_pieces, group * n_blk), n_blocks, items, n_items


def home_tables(slot, group, n_chunks, starts):
    n_exp, tokens = slot.shape
    local = n_exp // group
    n_blk = tokens // TBLK
    slot = slot.reshape(group, local, n_blk, TBLK)
    chunk = jnp.where(slot >= 0, slot // PART, -1)
    active = jnp.any(chunk == jnp.arange(n_chunks, dtype=I32)[:, N, N, N, N], axis=(2, 4))
    chunks, n_used = compact(active.transpose(2, 0, 1).reshape(n_blk, n_chunks * group))
    last = jnp.max(piece_of(slot, starts), axis=(0, 1, 3))
    blocks, n_ready = compact(last == jnp.arange(len(starts), dtype=I32)[:, N])
    return chunks, n_used, blocks, n_ready


def expert_kernel(pos_ref, inv_ref, first_ref, blk_ref, nblk_ref, item_ref, info_ref, slot_ref, *refs, n_req, n_out, n_slots, base, stride):
    u_refs = refs[:n_req]
    wg_hbm, wu_hbm, wd_hbm = refs[n_req:n_req + 3]
    outs = refs[n_req + 3:n_req + 3 + n_out]
    trash, wgu, wdn, rows_ref, acc, ubuf, obuf, zbuf, wsem, usem, osem, zsem = refs[n_req + 3 + n_out:]
    local, _, ff = wg_hbm.shape
    piece = acc.shape[0]
    per = piece // UNIT
    tile = obuf.shape[1]
    tile_units = tile // UNIT
    n_blk = slot_ref.shape[1] // TBLK
    n_grp = n_blk // GROUP_BLKS
    req_blk = n_blk // n_slots
    n_items = info_ref[0]

    def weights(exp, slot):
        return (
            pltpu.make_async_copy(wg_hbm.at[exp], wgu.at[slot, :, pl.ds(0, ff)], wsem.at[slot, 0]),
            pltpu.make_async_copy(wu_hbm.at[exp], wgu.at[slot, :, pl.ds(ff, ff)], wsem.at[slot, 1]),
            pltpu.make_async_copy(wd_hbm.at[exp], wdn.at[slot], wsem.at[slot, 2]),
        )

    def each_block(index, todo):
        item = item_ref[index]
        src, grp = item // n_grp, item % n_grp
        for part in range(GROUP_BLKS):
            place = grp * GROUP_BLKS + part

            @pl.when(place < nblk_ref[src])
            def _():
                todo(src, blk_ref[src * n_blk + place], part)

    def fetch(index):
        side = index % 2

        def one(src, blk, part):
            start = pl.multiple_of((src * req_blk + blk % req_blk) * TBLK, TBLK)
            for req in range(n_req):
                @pl.when(blk // req_blk == req)
                def _():
                    pltpu.make_async_copy(u_refs[req].at[pl.ds(start, TBLK), :], ubuf.at[side, pl.ds(part * TBLK, TBLK), :], usem.at[side]).start()

        each_block(index, one)

    def fetched(index):
        side = index % 2

        def one(src, blk, part):
            pltpu.make_async_copy(u_refs[0].at[pl.ds(0, TBLK), :], ubuf.at[side, pl.ds(part * TBLK, TBLK), :], usem.at[side]).wait()

        each_block(index, one)

    def unit_rows(unit):
        return pl.ds(pl.multiple_of(unit * UNIT, UNIT), UNIT)

    def send(src_ref, unit, sem):
        src, place = unit // stride, unit % stride
        each = per // n_out
        for part in range(n_out):
            @pl.when(place // each == part)
            def _():
                pltpu.make_async_copy(src_ref, outs[part].at[unit_rows(src * each + place % each)], sem).start()

    @pl.when(n_items > 0)
    def _():
        ubuf[...] = jnp.zeros_like(ubuf)
        fetch(0)
        for copy in weights(0, 0):
            copy.start()

    zbuf[...] = jnp.zeros_like(zbuf)
    used, whole = first_ref[local], first_ref[local + 1]

    def blank(index, carry):
        send(zbuf, inv_ref[index], zsem)
        return carry

    lax.fori_loop(used, whole, blank, 0)

    def gather(index, carry):
        item = item_ref[index]
        src, grp = item // n_grp, item % n_grp
        side = index % 2

        @pl.when(index + 1 < n_items)
        def _():
            fetch(index + 1)

        row = lax.broadcasted_iota(I32, (piece, TBLK), 0)
        picks = []
        for part in range(GROUP_BLKS):
            place = grp * GROUP_BLKS + part
            blk = blk_ref[src * n_blk + jnp.minimum(place, n_blk - 1)]
            at = slot_ref[pl.ds(pl.multiple_of(src * local, local), local), pl.ds(pl.multiple_of(blk * TBLK, TBLK), TBLK)] - base
            at = jnp.where(place < nblk_ref[src], at, -1)
            pick = jnp.zeros((piece, TBLK), F32)
            for exp in range(local):
                pick = jnp.where(at[exp:exp + 1, :] == row, 1.0, pick)
            picks.append(pick.astype(BF16))
        pick = jnp.concatenate(picks, axis=1)
        fetched(index)

        @pl.when(grp == 0)
        def _():
            acc[...] = dot(pick, ubuf[side])

        @pl.when(grp > 0)
        def _():
            acc[...] += dot(pick, ubuf[side])

        @pl.when((grp + 1) * GROUP_BLKS >= nblk_ref[src])
        def _():
            for unit in range(per):
                rows_ref[unit_rows(pos_ref[src * stride + unit]), :] = acc[unit * UNIT:(unit + 1) * UNIT, :].astype(BF16)

        return carry

    lax.fori_loop(0, n_items, gather, 0)

    def store(slot):
        return pltpu.make_async_copy(obuf.at[slot], trash.at[slot], osem.at[slot])

    def expert(exp, done):
        slot = exp % 2

        @pl.when(exp + 1 < local)
        def _():
            for copy in weights(exp + 1, 1 - slot):
                copy.start()

        for copy in weights(exp, slot):
            copy.wait()
        begin, end = first_ref[exp], first_ref[exp + 1]

        def one_tile(index, done):
            unit0 = begin + index * tile_units
            x_val = rows_ref[pl.ds(pl.multiple_of(unit0 * UNIT, UNIT), tile), :]
            hid = dot(x_val, wgu[slot])
            gate = hid[:, :ff]
            act = (gate * jax.nn.sigmoid(gate) * hid[:, ff:]).astype(BF16)
            side = done % 2

            @pl.when(done >= 2)
            def _():
                store(side).wait()

            obuf[side] = dot(act, wdn[slot]).astype(BF16)

            def out(unit, carry):
                src_ref = obuf.at[side, unit_rows(unit), :]

                @pl.when(unit0 + unit < end)
                def _():
                    send(src_ref, inv_ref[unit0 + unit], osem.at[side])

                @pl.when(unit0 + unit >= end)
                def _():
                    pltpu.make_async_copy(src_ref, trash.at[side, unit_rows(unit), :], osem.at[side]).start()

                return carry

            lax.fori_loop(0, tile_units, out, 0)
            return done + 1

        return lax.fori_loop(0, (end - begin + tile_units - 1) // tile_units, one_tile, done)

    done = lax.fori_loop(0, jnp.where(n_items > 0, local, 0), expert, 0)
    for side in range(2):
        @pl.when(done > side)
        def _():
            store(side).wait()

    def blank_wait(index, carry):
        pltpu.make_async_copy(zbuf, outs[0].at[pl.ds(0, UNIT), :], zsem).wait()
        return carry

    lax.fori_loop(used, whole, blank_wait, 0)


def experts(index, tables, slots, gathered, w_gate, w_up, w_down, start, size, n_out):
    pos, inv, first, blocks, n_blocks, items, n_items = tables
    group, local, tokens = slots.shape
    n_req = len(gathered)
    _, width, ff = w_gate.shape
    tile = PIECE
    rows = group * size
    kernel = functools.partial(expert_kernel, n_req=n_req, n_out=n_out, n_slots=tokens * group // gathered[0].shape[0], base=start, stride=pos.shape[1] // group)
    outs = pl.pallas_call(
        kernel,
        grid_spec=pltpu.PrefetchScalarGridSpec(
            num_scalar_prefetch=7,
            grid=(1,),
            in_specs=[whole_spec((group * local, tokens))] + [pl.BlockSpec(memory_space=ANY)] * (n_req + 3),
            out_specs=[pl.BlockSpec(memory_space=ANY)] * (n_out + 1),
            scratch_shapes=[
                VMEM((2, width, 2 * ff), BF16),
                VMEM((2, ff, width), BF16),
                VMEM((rows + tile, width), BF16),
                VMEM((size, width), F32),
                VMEM((2, GROUP_BLKS * TBLK, width), BF16),
                VMEM((2, tile, width), BF16),
                VMEM((UNIT, width), BF16),
                pltpu.SemaphoreType.DMA((2, 3)),
                pltpu.SemaphoreType.DMA((2,)),
                pltpu.SemaphoreType.DMA((2,)),
                pltpu.SemaphoreType.DMA,
            ],
        ),
        out_shape=[jax.ShapeDtypeStruct((rows // n_out, width), BF16)] * n_out + [jax.ShapeDtypeStruct((2, tile, width), BF16)],
        compiler_params=pltpu.CompilerParams(vmem_limit_bytes=62 * MIB),
        cost_estimate=pl.CostEstimate(flops=6 * rows * width * ff, bytes_accessed=6 * local * width * ff, transcendentals=rows * ff),
    )(pos[index], inv[index], first[index], blocks[index], n_blocks[index], items[index], n_items[index:index + 1], slots.reshape(group * local, tokens), *gathered, w_gate, w_up, w_down)
    return [out.reshape(group, size // n_out, width) for out in outs[:n_out]]


def sum_kernel(blk_ref, nblk_ref, used_ref, chunk_ref, len_ref, turn_ref, slot_ref, prob_ref, *refs, n_req, n_back, n_chunks):
    totals, backs = refs[:n_req], refs[n_req:n_req + n_back]
    y_hbm, gates, rbuf, tbuf, acc, ybuf, todo_ref, rsem, tsem, ysem = refs[n_req + n_back + 1:]
    depth = rbuf.shape[0]
    n_exp = slot_ref.shape[0]
    width = tbuf.shape[2]
    n_blk = slot_ref.shape[1] // TBLK
    req_blk = n_blk // n_req
    group = backs[0].shape[0]
    local = n_exp // group
    n_ready = nblk_ref[0]
    per_blk = group * n_chunks

    def each_chunk(blk, grp, todo):
        for part in range(GROUP_BLKS):
            place = grp * GROUP_BLKS + part

            @pl.when(place < used_ref[blk])
            def _():
                item = chunk_ref[blk * per_blk + place]
                todo(item // group, item % group, part)

    def fetch(blk, grp, side):
        def one(chunk, owner, part):
            first = 0
            for ref in backs:
                have = ref.shape[1] // PART
                lo = first

                @pl.when((chunk >= lo) & (chunk < lo + have))
                def _():
                    start = pl.multiple_of((chunk - lo) * PART, PART)
                    pltpu.make_async_copy(ref.at[owner, pl.ds(start, PART), :], rbuf.at[side, pl.ds(part * PART, PART), :], rsem.at[side]).start()

                first += have

        each_chunk(blk, grp, one)

    def fetched(blk, grp, side):
        each_chunk(blk, grp, lambda chunk, owner, part: pltpu.make_async_copy(backs[0].at[0, pl.ds(0, PART), :], rbuf.at[side, pl.ds(part * PART, PART), :], rsem.at[side]).wait())

    def total_start(blk, side):
        rows = pl.ds(pl.multiple_of(blk % req_blk * TBLK, TBLK), TBLK)
        for req in range(n_req):
            @pl.when(blk // req_blk == req)
            def _():
                pltpu.make_async_copy(totals[req].at[rows, :], tbuf.at[side], tsem.at[side]).start()

    def y_copy(blk, side):
        start = (turn_ref[blk // req_blk] * req_blk + blk % req_blk) * TBLK
        return pltpu.make_async_copy(ybuf.at[side], y_hbm.at[pl.ds(pl.multiple_of(start, TBLK), TBLK), :], ysem.at[side])

    def at_item(index):
        item = todo_ref[index]
        return item // per_blk, item % per_blk

    def prefetch(index):
        @pl.when(index < n_items)
        def _():
            place, grp = at_item(index)
            fetch(blk_ref[place], grp, index % depth)

    def groups(index):
        return (used_ref[blk_ref[index]] + GROUP_BLKS - 1) // GROUP_BLKS

    def list_block(index, count):
        def one(grp, count):
            todo_ref[count] = index * per_blk + grp
            return count + 1

        return lax.fori_loop(0, groups(index), one, count)

    n_items = lax.fori_loop(0, n_ready, list_block, 0)

    @pl.when(n_ready > 0)
    def _():
        total_start(blk_ref[0], 0)
        rbuf[...] = jnp.zeros_like(rbuf)
        for index in range(depth - 1):
            prefetch(index)

    def step(index, carry):
        order, grp = at_item(index)
        blk = blk_ref[order]
        side = order % 2
        hand = index % depth
        cols = pl.ds(pl.multiple_of(blk * TBLK, TBLK), TBLK)
        prefetch(index + depth - 1)

        @pl.when(grp == 0)
        def _():
            pltpu.make_async_copy(totals[0].at[pl.ds(0, TBLK), :], tbuf.at[side], tsem.at[side]).wait()

            @pl.when(order + 1 < n_ready)
            def _():
                total_start(blk_ref[order + 1], 1 - side)

            acc[...] = tbuf[side]

        row = lax.broadcasted_iota(I32, (PART, TBLK), 0)
        for part in range(GROUP_BLKS):
            place = grp * GROUP_BLKS + part
            item = chunk_ref[blk * per_blk + jnp.minimum(place, per_blk - 1)]
            chunk, owner = item // group, item % group
            own = pl.ds(pl.multiple_of(owner * local, local), local)
            at = jnp.where(place < used_ref[blk], slot_ref[own, cols] - chunk * PART, -1)
            prob = prob_ref[own, cols]
            gate = jnp.zeros((PART, TBLK), F32)
            for exp in range(local):
                gate = jnp.where(at[exp:exp + 1, :] == row, prob[exp:exp + 1, :], gate)
            rows = slice(part * PART, (part + 1) * PART)
            for term in range(TERMS):
                high = gate.astype(BF16)
                gates[rows, term * TBLK:(term + 1) * TBLK] = high
                gate = gate - high.astype(F32)
        fetched(blk, grp, hand)
        for start in range(0, width, COLS):
            at = slice(start, start + COLS)
            out = lax.dot_general(gates[...], rbuf[hand, :, at], FIRST_DIMS, preferred_element_type=F32)
            acc[:, at] += sum(out[term * TBLK:(term + 1) * TBLK] for term in range(TERMS))

        @pl.when(grp + 1 == groups(order))
        def _():
            @pl.when(order >= 2)
            def _():
                y_copy(blk, side).wait()

            keep = len_ref[blk // req_blk] - (blk % req_blk) * TBLK
            good = lax.broadcasted_iota(I32, (TBLK, 1), 0) < keep
            ybuf[side] = jnp.where(good, acc[...], 0.0).astype(BF16)
            y_copy(blk, side).start()

        return carry

    lax.fori_loop(0, n_items, step, 0)
    for back in range(1, 3):
        @pl.when(n_ready >= back)
        def _():
            y_copy(0, (n_ready - back) % 2).wait()


def sum_ready(index, home, lens, turn, slot, prob, totals, backs, y_buf):
    chunks, n_used, blocks, n_ready = home
    n_exp, tokens = slot.shape
    group, _, width = backs[0].shape
    n_back, n_req = len(backs), len(totals)
    n_chunks = chunks.shape[1] // group
    (y_buf,) = pl.pallas_call(
        functools.partial(sum_kernel, n_req=n_req, n_back=n_back, n_chunks=n_chunks),
        grid_spec=pltpu.PrefetchScalarGridSpec(
            num_scalar_prefetch=6,
            grid=(1,),
            in_specs=[whole_spec((n_exp, tokens)), whole_spec((n_exp, tokens))] + [pl.BlockSpec(memory_space=ANY)] * (n_req + n_back + 1),
            out_specs=[pl.BlockSpec(memory_space=ANY)],
            scratch_shapes=[
                VMEM((GROUP_BLKS * PART, TERMS * TBLK), BF16),
                VMEM((3, GROUP_BLKS * PART, width), BF16),
                VMEM((2, TBLK, width), F32),
                VMEM((TBLK, width), F32),
                VMEM((2, TBLK, width), BF16),
                pltpu.SMEM((chunks.size // GROUP_BLKS + tokens // TBLK,), I32),
                pltpu.SemaphoreType.DMA((3,)),
                pltpu.SemaphoreType.DMA((2,)),
                pltpu.SemaphoreType.DMA((2,)),
            ],
        ),
        out_shape=[jax.ShapeDtypeStruct(y_buf.shape, BF16)],
        input_output_aliases={8 + n_req + n_back: 0},
        compiler_params=pltpu.CompilerParams(vmem_limit_bytes=40 * MIB),
        cost_estimate=pl.CostEstimate(flops=tokens * tokens * width, bytes_accessed=16 * MIB, transcendentals=0),
    )(blocks[index], n_ready[index:index + 1], n_used, chunks.reshape(-1), lens, turn, slot, prob, *totals, *backs, y_buf)
    return y_buf


def solution(mesh):
    group = mesh.shape['dpa']
    tok_spec = P(('dp', 'dpa'))
    whole = P()
    exp_spec = P('dpa')

    def after(value, *others):
        return lax.optimization_barrier((value,) + others)[0]

    def device_step(x_in, chunk_len, ctx_len, lat_cache, rope_cache, topk_idx, g_attn, w_q, w_dkv, g_kv, w_kr, w_uk, w_uv, w_o, g_ffn, w_router, w_sh_gate, w_sh_up, w_sh_down, w_exp_gate, w_exp_up, w_exp_down):
        _, n_req, chunk, width = x_in.shape
        rope = w_kr.shape[1]
        half = rope // 2
        heads, vdim = w_o.shape[:2]
        tokens = n_req * chunk
        top_k = topk_idx.shape[-1]
        n_exp = w_router.shape[1]
        local = n_exp // group
        capacity = tokens * top_k // group
        cap_rows = (capacity // UNIT + local) * UNIT
        starts = [index * PIECE for index in range(FIXED)] + [FIXED * PIECE]
        tail_parts = max(-(-(cap_rows - FIXED * PIECE) // PART), 1)
        near = (tail_parts + 1) // 2
        starts.append((FIXED + 0) * PIECE + near * PART)
        sizes = [PIECE] * FIXED + [near * PART, (tail_parts - near) * PART]
        lens, ctx = chunk_len[0], ctx_len[0]
        x_all = x_in[0]

        ids = jnp.arange(n_req, dtype=I32)
        ahead = (lens < lens[:, N]) | ((lens == lens[:, N]) & (ids < ids[:, N]))
        chosen = jnp.sum(ahead.astype(I32), axis=1) == ids[:, N]
        turn, lens_t, ctx_t = (jnp.sum(jnp.where(chosen, vals, 0), axis=1) for vals in (ids, lens, ctx))

        inv_freq = THETA ** (-2.0 * jnp.arange(half, dtype=F32) / rope)
        angle = inv_freq[:, N] * (ctx[:, N] + jnp.arange(chunk)).astype(F32)[:, N, :]
        cos_tab = jnp.concatenate([jnp.cos(angle), jnp.cos(angle)], axis=1)
        sin_tab = jnp.concatenate([-jnp.sin(angle), jnp.sin(angle)], axis=1)
        wuk = w_uk.transpose(1, 2, 0)
        wuv = w_uv.transpose(1, 0, 2)
        wo = w_o.reshape(heads * vdim, width)
        lat_all, rope_all = lat_cache[0], rope_cache[0].transpose(0, 2, 1)
        gathered, us, hs = [], [], []
        for index in range(n_req):
            x_req = lax.dynamic_index_in_dim(x_all, turn[index], keepdims=False)
            if us:
                x_req = after(x_req, us[-1])
            a_req = rms_norm(x_req, g_attn)
            q_req = jnp.einsum('cd,dhq->hqc', a_req, w_q, preferred_element_type=F32).astype(BF16)
            info = jnp.stack([lens_t[index], ctx_t[index], turn[index]])
            h_req, u_req, lat_all, rope_all = attention(info, x_all, a_req, q_req, wuk, wuv, w_dkv, w_kr, cos_tab, sin_tab, g_kv[N], g_ffn[N], wo, lat_all, rope_all)
            gathered.append(lax.all_gather(u_req, 'dpa', axis=0, tiled=True))
            us.append(u_req)
            hs.append(h_req)

        topk = after(topk_idx[0], us[0])
        topk = jnp.sum(jnp.where(chosen[:, :, N, N], topk, 0), axis=1).reshape(tokens, top_k)
        valid = (jnp.arange(chunk) < lens_t[:, N]).reshape(tokens)
        slot, n_units = slot_table(topk, valid, n_exp, group)
        slots = lax.all_to_all(slot.reshape(group, local, tokens), 'dpa', 0, 0, tiled=True)
        most = lax.pmax(jnp.max(n_units), 'dpa') * UNIT
        tables = owner_tables(slots, starts, sizes)
        head = min(EARLY, n_req)
        late_rows = slots[:, :, head * chunk:]
        early = jnp.logical_not(jnp.any((late_rows >= 0) & (late_rows < PIECE)))
        start = after(tables[0], most)

        def run(index, start, feeds, n_out):
            return experts(index, (start,) + tables[1:], slots, feeds, w_exp_gate, w_exp_up, w_exp_down, starts[index], sizes[index], n_out)

        first = lax.cond(early, lambda: run(0, start, gathered[:head], 1)[0], lambda: jnp.zeros((group, PIECE, width), BF16))
        first = lax.cond(early, lambda rows: rows, lambda rows: run(0, start, gathered, 1)[0], first)
        backs, totals, probs = [], [], []

        def share(req, mark):
            total, prob = shared(after(lens_t, mark)[req:req + 1], us[req], hs[req], w_router, w_sh_gate, w_sh_up, w_sh_down)
            totals.append(total)
            probs.append(prob)
            return prob

        mark = first
        for index in range(FIXED):
            sent = first
            if index:
                sent = run(index, after(tables[0], mark), gathered, 1)[0]
                mark = sent
                if index <= n_req:
                    mark = share(index - 1, sent)
                    sent = after(sent, mark)
            backs.append(lax.all_to_all(sent, 'dpa', 0, 0, tiled=True))
        home = home_tables(slot, group, sum(sizes) // PART, starts[:-1])
        start = after(tables[0], mark)
        tail = run(FIXED, start, gathered, near)
        mark = tail[0]
        for req in range(len(totals), n_req):
            mark = share(req, mark)
        prob = jnp.concatenate(probs, axis=1)
        y_buf = jnp.zeros((tokens, width), BF16)

        def add(index, backs, y_buf):
            return sum_ready(index, home, lens_t, turn, slot, prob, totals, backs, y_buf)

        for index in range(FIXED - 2):
            y_buf = add(index, backs[:index + 1], y_buf)

        def send(rows):
            return lax.all_to_all(rows, 'dpa', 0, 0, tiled=True)

        fixed = list(backs)
        for index in range(near):
            done = FIXED - 2 + index
            rows = after(tail[index], backs[-1], y_buf)
            if done < FIXED:
                def sums(y):
                    return add(done, fixed[:done + 1], y)

                extra, y_buf = lax.cond(most > FIXED * PIECE + index * PART, lambda rows, y: (send(rows), sums(y)), lambda rows, y: (rows, sums(y)), rows, y_buf)
            else:
                extra = lax.cond(most > FIXED * PIECE + index * PART, send, lambda rows: rows, rows)
            backs.append(extra)
        if sizes[-1]:
            backs.append(lax.cond(
                most > starts[-1],
                lambda start: send(run(FIXED + 1, start, gathered, 1)[0]),
                lambda start: jnp.zeros((group, sizes[-1], width), BF16),
                after(start, backs[-1])))
        y_buf = add(FIXED, backs, y_buf)
        return y_buf.reshape(x_in.shape), lat_all[N], rope_all.transpose(0, 2, 1)[N]

    return jax.shard_map(device_step, mesh=mesh, in_specs=(tok_spec,) * 6 + (whole,) * 13 + (exp_spec,) * 3, out_specs=(tok_spec, tok_spec, tok_spec), check_vma=False)
```

time: 3330 us -> 1390 us (0.42)
  the two profiles are of different devices: /device:TPU:112 before, /device:TPU:122 now
where the time goes in v2:
time: 1390 us; the launch traced here: 1380 us
  Pallas kernels  865 us (62%)
  waiting for transfers between devices  134 us (10%)
  starting transfers between devices  122 us (9%)
  local copies, waits for them, and re-layouts  73.9 us (5%)
  blocking collectives  70.9 us (5%)
  other arithmetic  49.5 us (4%)
  matrix products  43.7 us (3%)
  between operations  25.1 us (2%)
    pallas_call x5, Pallas kernels, experts(): pl.pallas_call(kernel, grid_spec=pltpu.PrefetchScalarGridSpec(num_scalar_...  404 us
    pallas_call x4, Pallas kernels, attention(): pl.pallas_call(kernel, grid_spec=pltpu.PrefetchScalarGridSpec(num_scalar_...  184 us
    pallas_call x5, Pallas kernels, sum_ready(): pl.pallas_call(functools.partial(sum_kernel, n_req=n_req, n_back=n_back,...  149 us
    pallas_call x4, Pallas kernels, shared(): pl.pallas_call(shared_kernel, grid_spec=pltpu.PrefetchScalarGridSpec(num_...  128 us
    all_to_all x4, starting transfers between devices, device_step(): backs.append(lax.all_to_all(sent, 'dpa', 0, 0, tiled=True))  96.6 us
    all_to_all x4, waiting for transfers between devices, device_step(): backs.append(lax.all_to_all(sent, 'dpa', 0, 0, tiled=True))  83.7 us
    all_to_all x1, blocking collectives, send(): return lax.all_to_all(rows, 'dpa', 0, 0, tiled=True)  53.6 us
    unnamed x4, matrix products  40.9 us
  transfers between devices with their start and end apart: 11, of which 4 were waited for; matrix products, arithmetic and copies ran while one was open for 7% of the time, Pallas kernels for 55%

profile of v2, /device:TPU:122, one launch (start us, length us, event | category | flops | bytes accessed | tf_op | source)
XLA Modules:
  0.0 1384.7 jit_solution(8900370827443252134)
XLA Ops:
  9.2 4.6 copy.153
  29.5 10.1 fusion.63
  46.9 45.6 %shard_map.247 = (bf16[512,2048]{1,0:T(8,128)(2,1)}, bf16[512,2048]{1,0:T(8,128)(2,1)}, bf16[4,1024,512]{2,1,0:T(8,128)(2,1)}, bf16[4,64,1024]{2,1,0:T(8,128)(2,1)}) custom-call(s32[3]{0:T(128)} %pad_add_fusion.info, bf16[4,512,2048]{2,1,0:T(8,128)(2,1)} %bitcast.219, bf16[512,2048]{1,0:T(8,128)(2,1)} %copy-done.10, ...), custom_call_target="tpu_custom_call", output_to_operand_aliasing={{2}: (13, {}), {3}: (14, {})} | custom-call | flops 17179869184 | bytes 25165824 | tf_op jit(solution)/shard_map/pallas_call | solution.py:195
  98.4 5.9 dynamic-slice_bitcast_fusion
  107.9 10.1 fusion.64
  120.2 48.4 %shard_map.248 = (bf16[512,2048]{1,0:T(8,128)(2,1)}, bf16[512,2048]{1,0:T(8,128)(2,1)}, bf16[4,1024,512]{2,1,0:T(8,128)(2,1)}, bf16[4,64,1024]{2,1,0:T(8,128)(2,1)}) custom-call(s32[3]{0:T(128)} %pad_add_fusion.1.info, bf16[4,512,2048]{2,1,0:T(8,128)(2,1)} %bitcast.220, ...), custom_call_target="tpu_custom_call", output_to_operand_aliasing={{2}: (13, {}), {3}: (14, {})} | custom-call | flops 17179869184 | bytes 25165824 | tf_op jit(solution)/shard_map/pallas_call | solution.py:195
  175.6 10.5 fusion.65
  188.3 42.0 %shard_map.249 = (bf16[512,2048]{1,0:T(8,128)(2,1)}, bf16[512,2048]{1,0:T(8,128)(2,1)}, bf16[4,1024,512]{2,1,0:T(8,128)(2,1)}, bf16[4,64,1024]{2,1,0:T(8,128)(2,1)}) custom-call(s32[3]{0:T(128)} %pad_add_fusion.2.info, bf16[4,512,2048]{2,1,0:T(8,128)(2,1)} %bitcast.221, ...), custom_call_target="tpu_custom_call", output_to_operand_aliasing={{2}: (13, {}), {3}: (14, {})} | custom-call | flops 17179869184 | bytes 25165824 | tf_op jit(solution)/shard_map/pallas_call | solution.py:195
  233.8 10.1 fusion.66
  246.1 48.2 %shard_map.250 = (bf16[512,2048]{1,0:T(8,128)(2,1)}, bf16[512,2048]{1,0:T(8,128)(2,1)}, bf16[4,1024,512]{2,1,0:T(8,128)(2,1)}, bf16[4,64,1024]{2,1,0:T(8,128)(2,1)}) custom-call(s32[3]{0:T(128)} %pad_add_fusion.3.info, bf16[4,512,2048]{2,1,0:T(8,128)(2,1)} %bitcast.222, ...), custom_call_target="tpu_custom_call", output_to_operand_aliasing={{2}: (13, {}), {3}: (14, {})} | custom-call | flops 17179869184 | bytes 25165824 | tf_op jit(solution)/shard_map/pallas_call | solution.py:195
  304.6 3.6 all-to-all-start.4
  308.9 17.3 %pmax.7 = s32[]{:T(128)} all-reduce(s32[]{:T(128)} %reduce_max.19), channel_id=1, replica_groups=mesh['dp'=2,'dpa'=8] {'dpa'}, use_global_device_ids=true, to_apply=%region_27.28 | all-reduce | flops 1 | bytes 8 | tf_op jit(solution)/shard_map/pmax | solution.py:829
  335.1 9.6 all-gather.9.cloned.1.call-done.refs_2_
  344.7 85.0 %conditional.6 = (bf16[8,256,2048]{2,1,0:T(8,128)(2,1)}) conditional(s32[]{:T(128)} %convert_element_type.422, () %tuple.74, (s32[6,192]{1,0:T(8,128)S(1)}, s32[6,192]{1,0:T(8,128)S(1)}, s32[6,10]{0,1:T(8,128)S(1)}, s32[6,128]{1,0:T(8,128)S(1)}, s32[6,8]{1,0:T(8,128)S(1)}, /*index=5*/s32[6,32]{1,0:T(8,128)S(1)}, s32[6]{0:T(128)S(1)}, ...), branch_computations={%region_40.41_spmd, %region_41.42_spmd} | conditional | flops 35433480192 | bytes 138417024 | solution.py:839
  348.0 81.3 %branch_1_fun.4 = (bf16[2048,2048]{1,0:T(8,128)(2,1)}, bf16[2,256,2048]{2,1,0:T(8,128)(2,1)}) custom-call(s32[192]{0:T(256)} %bitcast.257, s32[192]{0:T(256)} %bitcast.256, s32[10]{0:T(128)} %slice_bitcast_fusion.3.first_ref, s32[128]{0:T(128)} %slice_bitcast_fusion.2.blk_ref, s32[8]{0:T(128)} %slice_bitcast_fusion.1.nblk_ref, ...), custom_call_target="tpu_custom_call" | custom-call | flops 35433480192 | bytes 138412032 | tf_op jit(solution)/shard_map/cond/branch_1_fun/pallas_call | solution.py:568
  429.7 8.4 conditional.7
  429.7 8.4 copy.131
  438.1 76.8 %all-to-all-start.5 = ((bf16[8,256,2048]{2,1,0:T(8,128)(2,1)}), bf16[8,256,2048]{2,1,0:T(8,128)(2,1)}, u32[]{:S(2)}, u32[]{:S(2)}) async-start(bf16[8,256,2048]{2,1,0:T(8,128)(2,1)} %get-tuple-element.653), calls=%async_computation.5 | async-start | bytes 16777216 | tf_op jit(solution)/shard_map/all_to_all | solution.py:858
  521.2 83.9 %shard_map.251 = (bf16[2048,2048]{1,0:T(8,128)(2,1)}, bf16[2,256,2048]{2,1,0:T(8,128)(2,1)}) custom-call(s32[192]{0:T(256)} %bitcast.264, s32[192]{0:T(256)} %bitcast.269, s32[10]{0:T(128)} %get-tuple-element.562.first_ref, s32[128]{0:T(128)} %squeeze.202.blk_ref, s32[8]{0:T(128)} %get-tuple-element.606.nblk_ref, s32[32]{0:T(128)} %get-tuple-element.602.item_ref, ...), custom_call_target="tpu_custom_call" | custom-call | flops 35433480192 | bytes 138412032 | tf_op jit(solution)/shard_map/pallas_call | solution.py:568
  605.1 31.7 %shard_map.252 = (f32[512,2048]{1,0:T(8,128)}, f32[64,512]{1,0:T(8,128)}) custom-call(s32[1]{0:T(128)S(1)} %bitcast.250, bf16[512,2048]{1,0:T(8,128)(2,1)} %get-tuple-element.417.u_ref, bf16[512,2048]{1,0:T(8,128)(2,1)} %get-tuple-element.435.h_ref, bf16[64,2048]{1,0:T(8,128)(2,1)} %bitcast.282, bf16[2048,2816]{1,0:T(8,128)(2,1)} %wg_hbm.7, ...), custom_call_target="tpu_custom_call" | custom-call | flops 17716740096 | bytes 34603008 | tf_op jit(solution)/shard_map/pallas_call | solution.py:282
  637.3 5.0 all-to-all-start.6
  642.4 89.0 %shard_map.253 = (bf16[2048,2048]{1,0:T(8,128)(2,1)}, bf16[2,256,2048]{2,1,0:T(8,128)(2,1)}) custom-call(s32[192]{0:T(256)} %bitcast.259, s32[192]{0:T(256)} %bitcast.268, s32[10]{0:T(128)} %get-tuple-element.561.first_ref, s32[128]{0:T(128)} %squeeze.208.blk_ref, s32[8]{0:T(128)} %get-tuple-element.605.nblk_ref, s32[32]{0:T(128)} %get-tuple-element.601.item_ref, ...), custom_call_target="tpu_custom_call" | custom-call | flops 35433480192 | bytes 138412032 | tf_op jit(solution)/shard_map/pallas_call | solution.py:568
  732.0 32.3 %shard_map.254 = (f32[512,2048]{1,0:T(8,128)}, f32[64,512]{1,0:T(8,128)}) custom-call(s32[1]{0:T(128)} %slice.314.lens, bf16[512,2048]{1,0:T(8,128)(2,1)} %get-tuple-element.423.u_ref, bf16[512,2048]{1,0:T(8,128)(2,1)} %get-tuple-element.440.h_ref, bf16[64,2048]{1,0:T(8,128)(2,1)} %bitcast.283, bf16[2048,2816]{1,0:T(8,128)(2,1)} %wg_hbm.7, ...), custom_call_target="tpu_custom_call" | custom-call | flops 17716740096 | bytes 34603008 | tf_op jit(solution)/shard_map/pallas_call | solution.py:282
  764.8 77.3 %shard_map.255 = (bf16[2048,2048]{1,0:T(8,128)(2,1)}, bf16[2,256,2048]{2,1,0:T(8,128)(2,1)}) custom-call(s32[192]{0:T(256)} %bitcast.265, s32[192]{0:T(256)} %bitcast.267, s32[10]{0:T(128)} %get-tuple-element.560.first_ref, s32[128]{0:T(128)} %squeeze.214.blk_ref, s32[8]{0:T(128)} %get-tuple-element.604.nblk_ref, s32[32]{0:T(128)} %get-tuple-element.600.item_ref, ...), custom_call_target="tpu_custom_call" | custom-call | flops 35433480192 | bytes 138412032 | tf_op jit(solution)/shard_map/pallas_call | solution.py:568
  842.7 32.2 %shard_map.256 = (f32[512,2048]{1,0:T(8,128)}, f32[64,512]{1,0:T(8,128)}) custom-call(s32[1]{0:T(128)} %slice.322.lens, bf16[512,2048]{1,0:T(8,128)(2,1)} %get-tuple-element.427.u_ref, bf16[512,2048]{1,0:T(8,128)(2,1)} %get-tuple-element.445.h_ref, bf16[64,2048]{1,0:T(8,128)(2,1)} %bitcast.284, bf16[2048,2816]{1,0:T(8,128)(2,1)} %wg_hbm.7, ...), custom_call_target="tpu_custom_call" | custom-call | flops 17716740096 | bytes 34603008 | tf_op jit(solution)/shard_map/pallas_call | solution.py:282
  875.3 8.4 all-to-all-start.8
  893.1 83.7 %all-to-all-done.8.refs_7_ = bf16[8,256,2048]{2,1,0:T(8,128)(2,1)} async-done(((bf16[8,256,2048]{2,1,0:T(8,128)(2,1)}), bf16[8,256,2048]{2,1,0:T(8,128)(2,1)}, u32[]{:S(2)}, u32[]{:S(2)}) %all-to-all-start.8) | async-done | bytes 8388640 | tf_op jit(solution)/shard_map/all_to_all | solution.py:858
  976.8 6.3 all-to-all-start.7
  983.2 72.9 %shard_map.257 = (bf16[1024,2048]{1,0:T(8,128)(2,1)}, bf16[1024,2048]{1,0:T(8,128)(2,1)}, bf16[1024,2048]{1,0:T(8,128)(2,1)}, bf16[2,256,2048]{2,1,0:T(8,128)(2,1)}) custom-call(s32[192]{0:T(256)} %bitcast.258, s32[192]{0:T(256)} %bitcast.266, s32[10]{0:T(128)} %get-tuple-element.559.first_ref, s32[128]{0:T(128)} %squeeze.220.blk_ref, ...), custom_call_target="tpu_custom_call" | custom-call | flops 53150220288 | bytes 138412032 | tf_op jit(solution)/shard_map/pallas_call | solution.py:568
  1056.8 32.2 %shard_map.258 = (f32[512,2048]{1,0:T(8,128)}, f32[64,512]{1,0:T(8,128)}) custom-call(s32[1]{0:T(128)} %slice.330.lens, bf16[512,2048]{1,0:T(8,128)(2,1)} %get-tuple-element.431.u_ref, bf16[512,2048]{1,0:T(8,128)(2,1)} %get-tuple-element.450.h_ref, bf16[64,2048]{1,0:T(8,128)(2,1)} %bitcast.285, bf16[2048,2816]{1,0:T(8,128)(2,1)} %wg_hbm.7, ...), custom_call_target="tpu_custom_call" | custom-call | flops 17716740096 | bytes 34603008 | tf_op jit(solution)/shard_map/pallas_call | solution.py:282
  1089.9 5.3 broadcast_in_dim.265.refs_5_
  1096.4 9.8 shard_map.259.refs_6_
  1106.2 24.8 %shard_map.260 = bf16[2048,2048]{1,0:T(8,128)(2,1)} custom-call(s32[16]{0:T(128)S(1)} %get-tuple-element.597.blk_ref, s32[1]{0:T(128)} %get-tuple-element.608.nblk_ref, s32[16]{0:T(128)S(1)} %convert_reduce_fusion.8.used_ref, s32[1664]{0:T(1024)S(1)} %reshape.1123.chunk_ref, s32[4]{0:T(128)S(1)} %copy-done.21, ...), custom_call_target="tpu_custom_call", output_to_operand_aliasing={{}: (14, {})} | custom-call | flops 8589934592 | bytes 16777216 | tf_op jit(solution)/shard_map/pallas_call | solution.py:743
  1131.0 68.8 %conditional.8 = (bf16[8,128,2048]{2,1,0:T(8,128)(2,1)}, bf16[2048,2048]{1,0:T(8,128)(2,1)}) conditional(s32[]{:T(128)} %convert_element_type.444, (s32[5,16]{1,0:T(8,128)S(1)}, s32[5]{0:T(128)S(1)}, s32[16,104]{1,0:T(8,128)S(1)}, s32[16]{0:T(128)S(1)}, s32[4]{0:T(128)S(1)}, /*index=5*/s32[4]{0:T(128)S(1)}, s32[64,2048]{1,0:T(8,128)S(1)}, ...), branch_computations={%region_44.45_spmd, %region_45.46_spmd} | conditional | flops 8589934592 | bytes 37762232 | solution.py:885
  1131.0 15.7 %all-to-all-start.1 = ((bf16[8,128,2048]{2,1,0:T(8,128)(2,1)}), bf16[8,128,2048]{2,1,0:T(8,128)(2,1)}, u32[]{:S(2)}, u32[]{:S(2)}) async-start(bf16[8,128,2048]{2,1,0:T(8,128)(2,1)} %get-tuple-element.291), calls=%async_computation.1 | async-start | bytes 8388608 | tf_op jit(solution)/shard_map/cond/branch_1_fun/all_to_all | solution.py:875
  1147.4 28.9 %branch_1_fun.5 = bf16[2048,2048]{1,0:T(8,128)(2,1)} custom-call(s32[16]{0:T(128)S(1)} %slice_bitcast_fusion.9.blk_ref, s32[1]{0:T(128)} %slice.203.nblk_ref, s32[16]{0:T(128)S(1)} %get-tuple-element.294.used_ref, s32[1664]{0:T(1024)S(1)} %reshape.1096.chunk_ref, s32[4]{0:T(128)S(1)} %get-tuple-element.296.len_ref, ...), custom_call_target="tpu_custom_call", output_to_operand_aliasing={{}: (15, {})} | custom-call | flops 8589934592 | bytes 16777216 | tf_op jit(solution)/shard_map/cond/branch_1_fun/pallas_call | solution.py:743
  1176.3 18.7 %all-to-all-done.1 = bf16[8,128,2048]{2,1,0:T(8,128)(2,1)} async-done(((bf16[8,128,2048]{2,1,0:T(8,128)(2,1)}), bf16[8,128,2048]{2,1,0:T(8,128)(2,1)}, u32[]{:S(2)}, u32[]{:S(2)}) %all-to-all-start.1) | async-done | bytes 4194336 | tf_op jit(solution)/shard_map/cond/branch_1_fun/all_to_all | solution.py:875
  1195.0 4.8 copy.139
  1199.8 59.1 %conditional.9 = (bf16[8,128,2048]{2,1,0:T(8,128)(2,1)}, bf16[2048,2048]{1,0:T(8,128)(2,1)}) conditional(s32[]{:T(128)} %convert_element_type.445, (s32[5,16]{1,0:T(8,128)S(1)}, s32[5]{0:T(128)S(1)}, s32[16,104]{1,0:T(8,128)S(1)}, s32[16]{0:T(128)S(1)}, s32[4]{0:T(128)S(1)}, /*index=5*/s32[4]{0:T(128)S(1)}, s32[64,2048]{1,0:T(8,128)S(1)}, ...), branch_computations={%region_46.47_spmd, %region_47.48_spmd} | conditional | flops 8589934592 | bytes 37762232 | solution.py:885
  1199.8 6.0 all-to-all-start.2
  1206.4 26.3 %branch_1_fun.6 = bf16[2048,2048]{1,0:T(8,128)(2,1)} custom-call(s32[16]{0:T(128)S(1)} %slice_bitcast_fusion.11.blk_ref, s32[1]{0:T(128)} %slice.207.nblk_ref, s32[16]{0:T(128)S(1)} %get-tuple-element.329.used_ref, s32[1664]{0:T(1024)S(1)} %reshape.1098.chunk_ref, s32[4]{0:T(128)S(1)} %get-tuple-element.331.len_ref, ...), custom_call_target="tpu_custom_call", output_to_operand_aliasing={{}: (16, {})} | custom-call | flops 8589934592 | bytes 16777216 | tf_op jit(solution)/shard_map/cond/branch_1_fun/pallas_call | solution.py:743
  1232.7 21.4 %all-to-all-done.2 = bf16[8,128,2048]{2,1,0:T(8,128)(2,1)} async-done(((bf16[8,128,2048]{2,1,0:T(8,128)(2,1)}), bf16[8,128,2048]{2,1,0:T(8,128)(2,1)}, u32[]{:S(2)}, u32[]{:S(2)}) %all-to-all-start.2) | async-done | bytes 4194336 | tf_op jit(solution)/shard_map/cond/branch_1_fun/all_to_all | solution.py:875
  1254.1 4.8 copy.143
  1258.9 55.8 %conditional.10 = (bf16[8,128,2048]{2,1,0:T(8,128)(2,1)}) conditional(s32[]{:T(128)} %convert_element_type.446, bf16[8,128,2048]{2,1,0:T(8,128)(2,1)} %bitcast.213, bf16[8,128,2048]{2,1,0:T(8,128)(2,1)} %bitcast.214), branch_computations={%region_48.49_spmd, %region_49.50_spmd} | conditional | bytes 25165860 | solution.py:887
  1261.1 53.6 %all_to_all.41 = bf16[8,128,2048]{2,1,0:T(8,128)(2,1)} all-to-all(bf16[8,128,2048]{2,1,0:T(8,128)(2,1)S(1)} %copy-done.4), channel_id=1, replica_groups=mesh['dp'=2,'dpa'=8] {'dpa'}, dimensions={0} | all-to-all | bytes 8388608 | tf_op jit(solution)/shard_map/cond/branch_1_fun/all_to_all | solution.py:875
  1314.7 4.3 conditional.11
  1314.7 4.3 broadcast.1208
  1319.0 58.8 %shard_map.261 = bf16[2048,2048]{1,0:T(8,128)(2,1)} custom-call(s32[16]{0:T(128)S(1)} %get-tuple-element.598.blk_ref, s32[1]{0:T(128)} %get-tuple-element.609.nblk_ref, s32[16]{0:T(128)S(1)} %convert_reduce_fusion.8.used_ref, s32[1664]{0:T(1024)S(1)} %reshape.1123.chunk_ref, s32[4]{0:T(128)S(1)} %copy-done.21, ...), custom_call_target="tpu_custom_call", output_to_operand_aliasing={{}: (20, {})} | custom-call | flops 8589934592 | bytes 16777216 | tf_op jit(solution)/shard_map/pallas_call | solution.py:743
  (430 shorter events, 88.7 us)
Async XLA Ops:
  7.2 327.9 %all-gather.5.cloned.1.call-start = ((), (), s32[]{:S(2)}) async-start(), calls=%async_computation.9 | async-start | bytes 18874368 | tf_op jit(solution)/shard_map/all_gather | solution.py:820
  14.2 281.2 %copy-start.20 = (s32[4]{0:T(128)}, s32[4]{0:T(128)S(1)}, u32[]{:S(2)}) copy-start(s32[4]{0:T(128)S(1)} %get-tuple-element.449.len_ref) | copy-start | bytes 52
  92.6 242.5 %all-gather.7.cloned.1.call-start = ((), (), s32[]{:S(2)}) async-start(), calls=%async_computation.10 | async-start | bytes 18874368 | tf_op jit(solution)/shard_map/all_gather | solution.py:820
  168.7 176.0 %all-gather.9.cloned.1.call-start = ((), (), s32[]{:S(2)}) async-start(), calls=%async_computation.11 | async-start | bytes 18874368 | tf_op jit(solution)/shard_map/all_gather | solution.py:820
  230.3 199.4 %all-gather.11.cloned.1.call-start = ((), (), s32[]{:S(2)}) async-start(), calls=%async_computation.12 | async-start | bytes 18874368 | tf_op jit(solution)/shard_map/all_gather | solution.py:820
  246.1 49.5 %copy-start.110 = (s32[4]{0:T(128)S(1)}, s32[4]{0:T(128)}, u32[]{:S(2)}) copy-start(s32[4]{0:T(128)} %copy-done.109) | copy-start | bytes 52
  246.1 49.5 %copy-start.26 = (s32[1,4,512,6]{2,1,3,0:T(4,128)S(1)}, s32[1,4,512,6]{2,1,3,0:T(4,128)}, u32[]{:S(2)}) copy-start(s32[1,4,512,6]{2,1,3,0:T(4,128)} %param.41) | copy-start | bytes 147460
  299.1 27.9 %copy-start.112 = (s32[6]{0:T(128)S(1)}, s32[6]{0:T(128)}, u32[]{:S(2)}) copy-start(s32[6]{0:T(128)} %constant.200) | copy-start | bytes 76
  302.0 42.7 %copy-start.5 = (s32[64,16,128]{2,1,0:T(8,128)}, s32[64,16,128]{2,1,0:T(8,128)S(1)}, u32[]{:S(2)}) copy-start(s32[64,16,128]{2,1,0:T(8,128)S(1)} %get-tuple-element.629) | copy-start | bytes 1572868
  304.6 22.5 %all-to-all-start.4 = ((s32[8,8,2048]{2,1,0:T(8,128)}), s32[8,8,2048]{2,1,0:T(8,128)S(1)}, u32[]{:S(2)}, u32[]{:S(2)}) async-start(s32[8,8,2048]{2,1,0:T(8,128)} %fusion.32), calls=%async_computation.4 | async-start | bytes 1048576 | tf_op jit(solution)/shard_map/all_to_all | solution.py:828
  330.2 188.6 %copy-start.25 = (s32[6,8]{1,0:T(8,128)}, s32[6,8]{1,0:T(8,128)S(1)}, u32[]{:S(2)}) copy-start(s32[6,8]{1,0:T(8,128)S(1)} %convert_reduce_fusion.10) | copy-start | bytes 580
  332.2 97.5 %copy-start.56 = (s32[6,128]{1,0:T(8,128)}, s32[6,128]{1,0:T(8,128)S(1)}, u32[]{:S(2)}) copy-start(s32[6,128]{1,0:T(8,128)S(1)} %reshape.1128) | copy-start | bytes 9220
  333.8 558.8 %copy-start.24 = (s32[6,192]{1,0:T(8,128)}, s32[6,192]{1,0:T(8,128)S(1)}, u32[]{:S(2)}) copy-start(s32[6,192]{1,0:T(8,128)S(1)} %convert_reduce_fusion) | copy-start | bytes 13828
  334.0 184.0 %copy-start.14 = (s32[6,10]{0,1:T(8,128)}, s32[6,10]{0,1:T(8,128)S(1)}, u32[]{:S(2)}) copy-start(s32[6,10]{0,1:T(8,128)S(1)} %convert_reduce_fusion.6) | copy-start | bytes 724
  334.3 183.1 %copy-start.30 = (s32[6]{0:T(128)}, s32[6]{0:T(128)S(1)}, u32[]{:S(2)}) copy-start(s32[6]{0:T(128)S(1)} %convert_reduce_fusion.9) | copy-start | bytes 76
  334.7 184.7 %copy-start.37 = (s32[6,32]{1,0:T(8,128)}, s32[6,32]{1,0:T(8,128)S(1)}, u32[]{:S(2)}) copy-start(s32[6,32]{1,0:T(8,128)S(1)} %select_reduce_fusion.6) | copy-start | bytes 2308
  335.0 185.0 %copy-start.29 = (s32[6,192]{1,0:T(8,128)}, s32[6,192]{1,0:T(8,128)S(1)}, u32[]{:S(2)}) copy-start(s32[6,192]{1,0:T(8,128)S(1)} %select_reduce_fusion) | copy-start | bytes 13828
  438.1 199.2 %all-to-all-start.5 = ((bf16[8,256,2048]{2,1,0:T(8,128)(2,1)}), bf16[8,256,2048]{2,1,0:T(8,128)(2,1)}, u32[]{:S(2)}, u32[]{:S(2)}) async-start(bf16[8,256,2048]{2,1,0:T(8,128)(2,1)} %get-tuple-element.653), calls=%async_computation.5 | async-start | bytes 16777216 | tf_op jit(solution)/shard_map/all_to_all | solution.py:858
  521.2 83.9 %copy-start.21 = (s32[4]{0:T(128)S(1)}, s32[4]{0:T(128)}, u32[]{:S(2)}) copy-start(s32[4]{0:T(128)} %copy-done.20) | copy-start | bytes 52
  637.3 238.0 %all-to-all-start.6 = ((bf16[8,256,2048]{2,1,0:T(8,128)(2,1)}), bf16[8,256,2048]{2,1,0:T(8,128)(2,1)}, u32[]{:S(2)}, u32[]{:S(2)}) async-start(bf16[8,256,2048]{2,1,0:T(8,128)(2,1)} %bitcast.225), calls=%async_computation.6 | async-start | bytes 16777216 | tf_op jit(solution)/shard_map/all_to_all | solution.py:858
  875.1 14.5 %copy-start.35 = (pred[16,16]{1,0:T(8,128)(4,1)S(1)}, pred[16,16]{1,0:T(8,128)(4,1)}, u32[]{:S(2)}) copy-start(pred[16,16]{1,0:T(8,128)(4,1)} %copy-done.34) | copy-start | bytes 772
  875.1 14.9 %copy-start.28 = (pred[2048]{0:T(1024)(128)(4,1)S(1)}, pred[2048]{0:T(1024)(128)(4,1)}, u32[]{:S(2)}) copy-start(pred[2048]{0:T(1024)(128)(4,1)} %copy-done.27) | copy-start | bytes 6148
  875.1 14.9 %copy-start.74 = (s32[64]{0:T(128)S(1)}, s32[64]{0:T(128)}, u32[]{:S(2)}) copy-start(s32[64]{0:T(128)} %copy-done.73) | copy-start | bytes 772
  875.2 14.9 %copy-start.76 = (s32[64]{0:T(128)S(1)}, s32[64]{0:T(128)}, u32[]{:S(2)}) copy-start(s32[64]{0:T(128)} %copy-done.75) | copy-start | bytes 772
  875.2 14.9 %copy-start.78 = (s32[64]{0:T(128)S(1)}, s32[64]{0:T(128)}, u32[]{:S(2)}) copy-start(s32[64]{0:T(128)} %copy-done.77) | copy-start | bytes 772
  875.2 14.9 %copy-start.80 = (s32[64]{0:T(128)S(1)}, s32[64]{0:T(128)}, u32[]{:S(2)}) copy-start(s32[64]{0:T(128)} %copy-done.79) | copy-start | bytes 772
  875.2 14.9 %copy-start.82 = (s32[64]{0:T(128)S(1)}, s32[64]{0:T(128)}, u32[]{:S(2)}) copy-start(s32[64]{0:T(128)} %copy-done.81) | copy-start | bytes 772
  875.2 14.9 %copy-start.84 = (s32[64]{0:T(128)S(1)}, s32[64]{0:T(128)}, u32[]{:S(2)}) copy-start(s32[64]{0:T(128)} %copy-done.83) | copy-start | bytes 772
  875.2 14.9 %copy-start.86 = (s32[64]{0:T(128)S(1)}, s32[64]{0:T(128)}, u32[]{:S(2)}) copy-start(s32[64]{0:T(128)} %copy-done.85) | copy-start | bytes 772
  875.2 14.9 %copy-start.88 = (s32[64]{0:T(128)S(1)}, s32[64]{0:T(128)}, u32[]{:S(2)}) copy-start(s32[64]{0:T(128)} %copy-done.87) | copy-start | bytes 772
  875.2 14.9 %copy-start.92 = (pred[64]{0:T(512)(128)(4,1)S(1)}, pred[64]{0:T(512)(128)(4,1)}, u32[]{:S(2)}) copy-start(pred[64]{0:T(512)(128)(4,1)} %copy-done.91) | copy-start | bytes 196
  875.2 14.9 %copy-start.94 = (pred[64]{0:T(512)(128)(4,1)S(1)}, pred[64]{0:T(512)(128)(4,1)}, u32[]{:S(2)}) copy-start(pred[64]{0:T(512)(128)(4,1)} %copy-done.93) | copy-start | bytes 196
  875.2 14.9 %copy-start.96 = (pred[64]{0:T(512)(128)(4,1)S(1)}, pred[64]{0:T(512)(128)(4,1)}, u32[]{:S(2)}) copy-start(pred[64]{0:T(512)(128)(4,1)} %copy-done.95) | copy-start | bytes 196
  875.3 14.9 %copy-start.98 = (pred[64]{0:T(512)(128)(4,1)S(1)}, pred[64]{0:T(512)(128)(4,1)}, u32[]{:S(2)}) copy-start(pred[64]{0:T(512)(128)(4,1)} %copy-done.97) | copy-start | bytes 196
  875.3 14.9 %copy-start.100 = (pred[64]{0:T(512)(128)(4,1)S(1)}, pred[64]{0:T(512)(128)(4,1)}, u32[]{:S(2)}) copy-start(pred[64]{0:T(512)(128)(4,1)} %copy-done.99) | copy-start | bytes 196
  875.3 14.9 %copy-start.102 = (pred[64]{0:T(512)(128)(4,1)S(1)}, pred[64]{0:T(512)(128)(4,1)}, u32[]{:S(2)}) copy-start(pred[64]{0:T(512)(128)(4,1)} %copy-done.101) | copy-start | bytes 196
  875.3 14.9 %copy-start.104 = (pred[64]{0:T(512)(128)(4,1)S(1)}, pred[64]{0:T(512)(128)(4,1)}, u32[]{:S(2)}) copy-start(pred[64]{0:T(512)(128)(4,1)} %copy-done.103) | copy-start | bytes 196
  875.3 14.9 %copy-start.106 = (pred[64]{0:T(512)(128)(4,1)S(1)}, pred[64]{0:T(512)(128)(4,1)}, u32[]{:S(2)}) copy-start(pred[64]{0:T(512)(128)(4,1)} %copy-done.105) | copy-start | bytes 196
  875.3 16.6 %copy-start.36 = (s32[1,8,16]{2,1,0:T(8,128)S(1)}, s32[1,8,16]{2,1,0:T(8,128)}, u32[]{:S(2)}) copy-start(s32[1,8,16]{2,1,0:T(8,128)} %get-tuple-element.583) | copy-start | bytes 1540
  875.3 101.5 %all-to-all-start.8 = ((bf16[8,256,2048]{2,1,0:T(8,128)(2,1)}), bf16[8,256,2048]{2,1,0:T(8,128)(2,1)}, u32[]{:S(2)}, u32[]{:S(2)}) async-start(bf16[8,256,2048]{2,1,0:T(8,128)(2,1)} %bitcast.224), calls=%async_computation.8 | async-start | bytes 16777216 | tf_op jit(solution)/shard_map/all_to_all | solution.py:858
  976.8 154.2 %all-to-all-start.7 = ((bf16[8,256,2048]{2,1,0:T(8,128)(2,1)}), bf16[8,256,2048]{2,1,0:T(8,128)(2,1)}, u32[]{:S(2)}, u32[]{:S(2)}) async-start(bf16[8,256,2048]{2,1,0:T(8,128)(2,1)} %bitcast.223), calls=%async_computation.7 | async-start | bytes 16777216 | tf_op jit(solution)/shard_map/all_to_all | solution.py:858
  983.1 73.5 %copy-start.17 = (f32[64,512]{1,0:T(8,128)S(1)}, f32[64,512]{1,0:T(8,128)}, u32[]{:S(2)}) copy-start(f32[64,512]{1,0:T(8,128)} %get-tuple-element.436) | copy-start | bytes 393220
  983.1 73.5 %copy-start.18 = (f32[64,512]{1,0:T(8,128)S(1)}, f32[64,512]{1,0:T(8,128)}, u32[]{:S(2)}) copy-start(f32[64,512]{1,0:T(8,128)} %get-tuple-element.441) | copy-start | bytes 393220
  983.2 73.6 %copy-start.19 = (f32[64,512]{1,0:T(8,128)S(1)}, f32[64,512]{1,0:T(8,128)}, u32[]{:S(2)}) copy-start(f32[64,512]{1,0:T(8,128)} %get-tuple-element.446) | copy-start | bytes 393220
  1131.0 64.0 %all-to-all-start.1 = ((bf16[8,128,2048]{2,1,0:T(8,128)(2,1)}), bf16[8,128,2048]{2,1,0:T(8,128)(2,1)}, u32[]{:S(2)}, u32[]{:S(2)}) async-start(bf16[8,128,2048]{2,1,0:T(8,128)(2,1)} %get-tuple-element.291), calls=%async_computation.1 | async-start | bytes 8388608 | tf_op jit(solution)/shard_map/cond/branch_1_fun/all_to_all | solution.py:875
  1199.8 54.3 %all-to-all-start.2 = ((bf16[8,128,2048]{2,1,0:T(8,128)(2,1)}), bf16[8,128,2048]{2,1,0:T(8,128)(2,1)}, u32[]{:S(2)}, u32[]{:S(2)}) async-start(bf16[8,128,2048]{2,1,0:T(8,128)(2,1)} %get-tuple-element.326), calls=%async_computation.2 | async-start | bytes 8388608 | tf_op jit(solution)/shard_map/cond/branch_1_fun/all_to_all | solution.py:875
  1258.9 55.8 %copy-start.15 = (s32[6,10]{0,1:T(8,128)S(1)}, s32[6,10]{0,1:T(8,128)}, u32[]{:S(2)}) copy-start(s32[6,10]{0,1:T(8,128)} %copy-done.14) | copy-start | bytes 724
  1258.9 55.8 %copy-start.31 = (s32[6]{0:T(128)S(1)}, s32[6]{0:T(128)}, u32[]{:S(2)}) copy-start(s32[6]{0:T(128)} %copy-done.30) | copy-start | bytes 76
  (76 other events, 543.1 us)
Sparse Core Ops, SparseCore 0:
  92.7 80.1 all-gather.4
  174.5 81.3 all-gather.6
  257.5 87.0 all-gather.8
  346.1 81.4 all-gather.10
